TPU v7x, 32 devices: a whole 2x2x4 slice. The times are simulated.
32 devices in a mesh: gx: 2 (over y), gy: 4 (over z), gz: 4 (over x, core).
Axes of the slice: x: 2, y: 2, z: 4, core: 2. Of those that a mesh axis runs over, the one named last changes fastest.
Arguments:
- section: float32 [25, 8, 64, 256], P(None, 'gz', 'gy', 'gx'), may hold values from -0.4 to 1.4, as said below
- base: float32 [25, 8, 64, 256], P(None, 'gz', 'gy', 'gx'), may hold values from -0.4 to 1.4, as said below
- accum: float32 [25, 8, 64, 256], P(None, 'gz', 'gy', 'gx'), may hold values from -4 to 4
Outputs:
- next_section: float32 [25, 8, 64, 256], P(None, 'gz', 'gy', 'gx')
- next_accum: float32 [25, 8, 64, 256], P(None, 'gz', 'gy', 'gx')
- slab: float32 [25, 8, 64, 256], P(None, 'gz')
Inputs may be any that keep to these rules, and one draw needn't show every extreme that they name: `section`: fields 0 and 17 (conformal factor and lapse) lie in 0.6 to 1.4; fields 1, 4 and 6 (the metric's diagonal) lie within 0.4 of 1; all other fields lie within 0.4 of 0. `base`: fields 0 and 17 (conformal factor and lapse) lie in 0.6 to 1.4; fields 1, 4 and 6 (the metric's diagonal) lie within 0.4 of 1; all other fields lie within 0.4 of 0.
All inputs are finite; a program needn't handle non-finite values.
Results may differ from a plain program's by a relative error of at most 0.0003.
Values sent between devices are 32-bit elements; how exact they have to be, the bound alone decides.
A program may use at most 64 MiB of HBM per device.

v0:
```python
import functools

import jax
import jax.numpy as jnp
from jax import lax
from jax.experimental import pallas as pl
from jax.experimental.pallas import tpu as pltpu
from jax.sharding import PartitionSpec as P

STEP_DT = 0.25
DISSIPATE = 0.1
DRIVER_ETA = 2.0
KAPPA_ONE = 0.1
PAIR_SLOT = ((0, 1, 2), (1, 3, 4), (2, 4, 5))
PAIR_LIST = ((0, 0), (0, 1), (0, 2), (1, 1), (1, 2), (2, 2))
MESH = pl.DeviceIdType.MESH
MIXED = (0, 17, 18, 19, 20)
RUNS = ((0, 1), (17, 4), (1, 5), (6, 2), (14, 3), (8, 5), (13, 1), (21, 4))
GROUPS = 5
ORDER = tuple(first + n for first, size in RUNS for n in range(size))
PLACE = tuple(ORDER.index(field) for field in range(len(ORDER)))
PAD = 8


def first_of(m2, m1, p1, p2):
    return (8.0 / 12.0) * (p1 - m1) - (1.0 / 12.0) * (p2 - m2)


def rates_of_plane(plane, rows, lanes, xb, tb, emit):
    lane = lax.broadcasted_iota(jnp.int32, (rows, lanes), 1)
    quad = lane & 3
    edge_one = (lane < 1) | (lane >= lanes - 1)
    edge_two = (lane < 2) | (lane >= lanes - 2)

    def cell(field, dz=0, dy=0):
        return xb[PLACE[field], plane + 2 + dz, PAD + dy : PAD + dy + rows, :]

    def strip(dz=0, dy=0):
        def side(slot):
            return tb[slot, plane + 2 + dz, PAD + dy : PAD + dy + rows, :]

        if tb.shape[0] == 1:
            return side(0)
        return jnp.where(quad < 2, side(1), side(0))

    def inner(edge):
        return jnp.where(
            quad == 1, pltpu.roll(edge, 1, 1), pltpu.roll(edge, lanes - 1, 1)
        )

    def x_line(field, value, edge, edge_in):
        turn = (lanes - 2 - 4 * field) % lanes
        two = pltpu.roll(edge, turn, 1)
        one = pltpu.roll(edge_in, turn, 1)
        m2 = jnp.where(edge_two & (lane < 64), two, pltpu.roll(value, 2, 1))
        m1 = jnp.where(edge_one & (lane < 64), one, pltpu.roll(value, 1, 1))
        p1 = jnp.where(edge_one & (lane >= 64), one, pltpu.roll(value, lanes - 1, 1))
        p2 = jnp.where(edge_two & (lane >= 64), two, pltpu.roll(value, lanes - 2, 1))
        return m2, m1, p1, p2

    def y_line(read):
        return tuple(read(0, dy) for dy in (-2, -1, 1, 2))

    def z_line(read):
        return tuple(read(dz, 0) for dz in (-2, -1, 1, 2))

    edge = strip()
    edge_in = inner(edge)
    edge_y = first_of(*y_line(strip))
    edge_y_in = inner(edge_y)
    edge_z = first_of(*z_line(strip))
    edge_z_in = inner(edge_z)

    centre, grad, curve, lap, mixed = {}, {}, {}, {}, {}
    need_lap = (0, 1, 2, 3, 4, 5, 6, 17, 18, 19, 20)
    shift = [cell(18), cell(19), cell(20)]
    advected = {}
    for field in range(len(ORDER)):
        centre[field] = cell(field)

    def differentiate(field):
        value = centre[field]
        read = functools.partial(cell, field)
        lines = [x_line(field, value, edge, edge_in), y_line(read), z_line(read)]
        near = [m1 + p1 for _, m1, p1, _ in lines]
        far = [m2 + p2 for m2, _, _, p2 in lines]
        near_sum = near[0] + near[1] + near[2]
        far_sum = far[0] + far[1] + far[2]
        smooth = far_sum - 4.0 * near_sum + 18.0 * value
        grads = [first_of(*line) for line in lines]
        grad[field] = grads
        advected[field] = (
            shift[0] * grads[0] + shift[1] * grads[1] + shift[2] * grads[2]
            - (DISSIPATE / 16.0) * smooth
        )
        if field in need_lap:
            lap[field] = (16.0 / 12.0) * near_sum - (1.0 / 12.0) * far_sum - 7.5 * value
        if field in MIXED:
            for axis in range(3):
                if field in (0, 17) or field == 18 + axis:
                    curve[field, axis] = (
                        (16.0 / 12.0) * near[axis] - (1.0 / 12.0) * far[axis] - 2.5 * value
                    )
            if field != 20:
                mixed[field, 0, 1] = first_of(*x_line(field, grads[1], edge_y, edge_y_in))
            if field != 19:
                mixed[field, 0, 2] = first_of(*x_line(field, grads[2], edge_z, edge_z_in))
            if field != 18:
                mixed[field, 1, 2] = first_of(
                    *(
                        first_of(*(cell(field, dz, dy) for dy in (-2, -1, 1, 2)))
                        for dz in (-2, -1, 1, 2)
                    )
                )

    def second(field, one, two):
        if one == two:
            return curve[field, one]
        return mixed[field, min(one, two), max(one, two)]

    def sym(table, one, two):
        return table[PAIR_SLOT[one][two]]

    metric = [centre[1 + k] for k in range(6)]
    traceless = [centre[8 + k] for k in range(6)]
    inverse = [
        (2.0 - metric[k]) if one == two else -metric[k]
        for k, (one, two) in enumerate(PAIR_LIST)
    ]

    def contract(left, right):
        diag = left[0] * right[0] + left[3] * right[3] + left[5] * right[5]
        off = left[1] * right[1] + left[2] * right[2] + left[4] * right[4]
        return diag + 2.0 * off

    def lie_of(table, one, two):
        total = None
        for k in range(3):
            if one == two:
                term = 2.0 * (sym(table, one, k) * grad[18 + k][one])
            else:
                term = (
                    sym(table, one, k) * grad[18 + k][two]
                    + sym(table, two, k) * grad[18 + k][one]
                )
            total = term if total is None else total + term
        return total

    group = len(ORDER) // GROUPS

    def begin(stage):
        for field in ORDER[stage * group : (stage + 1) * group]:
            differentiate(field)

    chi, trace, lapse, theta = centre[0], centre[7], centre[17], centre[24]

    begin(0)
    div = grad[18][0] + grad[19][1] + grad[20][2]
    third_div = (2.0 / 3.0) * div
    emit(0, advected[0] + (2.0 / 3.0) * chi * (lapse * trace) - chi * third_div)
    emit(17, advected[17] - 2.0 * lapse * (trace - 2.0 * theta))
    for one in range(3):
        emit(18 + one, advected[18 + one] + 0.75 * centre[21 + one])
    yield

    def metric_rate(k):
        one, two = PAIR_LIST[k]
        emit(
            1 + k,
            advected[1 + k]
            - 2.0 * lapse * traceless[k]
            + lie_of(metric, one, two)
            - metric[k] * third_div,
        )

    begin(1)
    for k in range(5):
        metric_rate(k)
    yield

    begin(2)
    metric_rate(5)
    over_chi = 1.0 / chi
    half_over = 0.5 * over_chi
    squares = contract(traceless, traceless)
    lapse_dd = [second(17, one, two) for one, two in PAIR_LIST]
    lapse_trace = contract(inverse, lapse_dd)
    emit(
        7,
        advected[7]
        - chi * lapse_trace
        + lapse * (squares + trace * trace * (1.0 / 3.0))
        + KAPPA_ONE * lapse * theta,
    )
    gauges = []
    for one in range(3):
        a_lapse = sum(sym(traceless, one, k) * grad[17][k] for k in range(3))
        a_chi = sum(sym(traceless, one, k) * grad[0][k] for k in range(3))
        g_trace = sum(sym(inverse, one, k) * grad[7][k] for k in range(3))
        b_mixed = sum(second(18 + k, one, k) for k in range(3))
        g_shift = sum(centre[14 + k] * grad[18 + one][k] for k in range(3))
        gauge = (
            -2.0 * a_lapse
            - lapse * ((4.0 / 3.0) * g_trace + 3.0 * (a_chi * over_chi))
            + lap[18 + one]
            + b_mixed * (1.0 / 3.0)
            + centre[14 + one] * third_div
            - g_shift
        )
        gauges.append(gauge)
        emit(14 + one, advected[14 + one] + gauge)
    yield

    begin(3)
    ricci = []
    for k, (one, two) in enumerate(PAIR_LIST):
        conf = second(0, one, two)
        if one == two:
            conf = conf + lap[0]
            grads_g = grad[14 + one][one]
        else:
            grads_g = 0.5 * (grad[14 + two][one] + grad[14 + one][two])
        ricci.append(-0.5 * lap[1 + k] + grads_g + conf * half_over)
    ricci_trace = contract(inverse, ricci)
    third_trace = (lapse * ricci_trace - lapse_trace) * (1.0 / 3.0)

    def traceless_rate(k):
        one, two = PAIR_LIST[k]
        free = lapse * ricci[k] - lapse_dd[k] - metric[k] * third_trace
        product = sum(
            sym(traceless, one, m) * sym(traceless, m, two) for m in range(3)
        )
        emit(
            8 + k,
            advected[8 + k]
            + chi * free
            + lapse * (trace * traceless[k] - 2.0 * product)
            + lie_of(traceless, one, two)
            - traceless[k] * third_div,
        )

    for k in range(5):
        traceless_rate(k)
    yield

    begin(4)
    traceless_rate(5)
    for one in range(3):
        emit(21 + one, advected[21 + one] + gauges[one] - DRIVER_ETA * centre[21 + one])
    emit(
        24,
        advected[24]
        + 0.5 * lapse * (chi * ricci_trace + (2.0 / 3.0) * trace * trace - squares)
        - 2.0 * KAPPA_ONE * lapse * theta,
    )
    yield


def section_kernel(
    sizes, groups, section, base, accum, ns_out, na_out, slab,
    xb, tb, tile, bb, ab, local_sem, halo_send, halo_recv,
    line_send, gather_recv,
):
    gx, gy, gz = sizes
    fields, planes, rows, lanes = section.shape
    i, j, k = (lax.axis_index(name) for name in ("gx", "gy", "gz"))
    group = fields // groups

    def device(dx=0, dy=0, dz=0):
        return (
            lax.rem(i + dx + gx, gx),
            lax.rem(j + dy + gy, gy),
            lax.rem(k + dz + gz, gz),
        )

    x_steps = (1,) if gx == 2 else (1, -1)
    messages = []

    def plane_pair(dz):
        if dz == 0:
            return slice(0, planes), slice(2, 2 + planes)
        if dz == 1:
            return slice(planes - 2, planes), slice(0, 2)
        return slice(0, 2), slice(2 + planes, 4 + planes)

    def row_pair(dy):
        if dy == 0:
            return slice(0, rows), slice(PAD, PAD + rows)
        if dy == 1:
            return slice(rows - 2, rows), slice(PAD - 2, PAD)
        return slice(0, 2), slice(PAD + rows, PAD + rows + 2)

    def at(ref, lead, plane_cut, row_cut):
        def ds(cut):
            return pl.ds(cut.start, cut.stop - cut.start)

        return ref.at[lead, ds(plane_cut), ds(row_cut), :]

    def own(cut_p, cut_r):
        return (
            slice(cut_p.start + 2, cut_p.stop + 2),
            slice(cut_r.start + PAD, cut_r.stop + PAD),
        )

    stages = [[] for _ in range(groups)]

    def add(stage, delta, src, dst):
        stages[stage].append(len(messages))
        messages.append((delta, src, dst))

    def face(stage, delta):
        src_p, dst_p = plane_pair(delta[2])
        src_r, dst_r = row_pair(delta[1])
        run = pl.ds(stage * group, group)
        add(stage, delta, at(xb, run, *own(src_p, src_r)), at(xb, run, dst_p, dst_r))

    for stage in range(groups):
        for step in (1, -1):
            face(stage, (0, step, 0))
            face(stage, (0, 0, step))
        if stage == 0:
            for dy in (1, -1):
                for dz in (1, -1):
                    face(0, (0, dy, dz))
    direct = len(messages)
    for slot, dx in enumerate(x_steps):
        for dy, dz in ((0, 0), (1, 0), (-1, 0), (0, 1), (0, -1)):
            src_p, dst_p = plane_pair(dz)
            src_r, dst_r = row_pair(dy)
            add(0, (dx, dy, dz), at(tile, 0, src_p, src_r), at(tb, slot, dst_p, dst_r))

    loads = []
    place = 0
    for first, size in RUNS:
        loads.append(
            pltpu.make_async_copy(
                section.at[pl.ds(first, size)],
                xb.at[pl.ds(place, size), pl.ds(2, planes), pl.ds(PAD, rows), :],
                local_sem.at[2 + len(loads)],
            )
        )
        place += size
    load_base = pltpu.make_async_copy(base, bb, local_sem.at[0])
    load_accum = pltpu.make_async_copy(accum, ab, local_sem.at[1])
    for load in loads:
        load.start()
    load_base.start()
    load_accum.start()

    partners = []
    for delta, _, _ in messages:
        if delta not in partners:
            partners.append(delta)
    barrier = pltpu.get_barrier_semaphore()
    for delta in partners:
        pl.semaphore_signal(barrier, inc=1, device_id=device(*delta), device_id_type=MESH)

    copies = [
        pltpu.make_async_remote_copy(
            src_ref=src, dst_ref=dst, send_sem=halo_send.at[m], recv_sem=halo_recv.at[m],
            device_id=device(*delta), device_id_type=MESH,
        )
        for m, (delta, src, dst) in enumerate(messages)
    ]
    for load in loads:
        load.wait()
    lane = lax.broadcasted_iota(jnp.int32, (rows, lanes), 1)

    def pack(plane, carry):
        packed = jnp.zeros((rows, lanes), jnp.float32)
        for field in range(fields):
            value = xb[PLACE[field], plane + 2, PAD : PAD + rows, :]
            ends = jnp.where(lane < 2, value, pltpu.roll(value, 4, 1))
            if field:
                ends = pltpu.roll(ends, 4 * field, 1)
            packed = jnp.where((lane >> 2) == field, ends, packed)
        tile[0, plane] = packed
        return carry

    lax.fori_loop(0, planes, pack, 0)
    pl.semaphore_wait(barrier, len(partners))
    def block(m):
        return messages[m][0][:2] == (0, 0)

    order = sorted(range(len(messages)), key=lambda m: (block(m), m < direct))
    for m in order:
        copies[m].start()
    load_base.wait()
    load_accum.wait()

    own_rows = pl.ds(pl.multiple_of(j * rows, rows), rows)
    own_cols = pl.ds(pl.multiple_of(i * lanes, lanes), lanes)

    def piece(ref, bi, bj, c=None):
        lead = pl.ds(0, fields) if c is None else pl.ds(c * group, group)
        return ref.at[
            lead,
            :,
            pl.ds(pl.multiple_of(bj * rows, rows), rows),
            pl.ds(pl.multiple_of(bi * lanes, lanes), lanes),
        ]

    towards = ((0, 1), (0, -1), (1, 0), (-1, 0))

    def send(link, bi, bj, c):
        dx, dy = towards[link]
        return pltpu.make_async_remote_copy(
            src_ref=piece(slab, bi, bj, c),
            dst_ref=piece(slab, bi, bj, c),
            send_sem=line_send.at[link, bi, bj, c],
            recv_sem=gather_recv.at[bi, bj, c],
            device_id=device(dx, dy, 0),
            device_id_type=MESH,
        )

    def arrive(bi, bj, c):
        part = piece(slab, bi, bj, c)
        pltpu.make_async_remote_copy(
            src_ref=part, dst_ref=part, send_sem=line_send.at[0, bi, bj, c],
            recv_sem=gather_recv.at[bi, bj, c], device_id=device(0, 1, 0),
            device_id_type=MESH,
        ).wait_recv()

    paired = gx == 2 and gy % 2 == 0
    turned = (groups * 2) // 5 if paired else 0
    pair = j + 1 - 2 * lax.rem(j, 2)

    def each(count, body, start=0):
        lax.fori_loop(start, count, lambda c, carry: (body(c), carry)[1], 0)

    def x_links(body):
        @pl.when(i + 1 < gx)
        def _():
            body(2)

        @pl.when(i > 0)
        def _():
            body(3)

    def send_own(c):
        @pl.when(j + 1 < gy)
        def _():
            send(0, i, j, c).start()

        @pl.when(j > 0)
        def _():
            send(1, i, j, c).start()

        x_links(lambda link: send(link, i, j, c).start())

    def emit_at(plane):
        def emit(field, rate):
            moved = bb[field, plane] + (0.5 * STEP_DT) * rate
            slab[PLACE[field], plane, own_rows, own_cols] = moved
            ns_out[field, plane] = moved
            na_out[field, plane] = ab[field, plane] + (STEP_DT / 3.0) * rate

        return emit

    def await_rows(stage, along_y):
        for m in stages[stage]:
            if (messages[m][0][2] == 0) == along_y:
                copies[m].wait_recv()

    await_rows(0, True)
    await_rows(0, False)
    work = [
        rates_of_plane(plane, rows, lanes, xb, tb, emit_at(plane))
        for plane in range(planes)
    ]
    for stage in range(groups):
        for part in work:
            next(part)
        if stage + 1 < groups:
            await_rows(stage + 1, True)
        send_own(stage)
        if stage + 1 < groups:
            await_rows(stage + 1, False)

    def crossed(d, bj, c, body):
        if d == 1 and turned:
            @pl.when((bj != pair) | (c >= turned))
            def _():
                body()
        else:
            body()

    other = 1 - i

    for d in range(1, gy):
        def column(c, d=d):
            @pl.when(j - d >= 0)
            def _():
                bj = j - d
                arrive(i, bj, c)

                @pl.when(j + 1 < gy)
                def _():
                    send(0, i, bj, c).start()

                crossed(d, bj, c, lambda: x_links(lambda link: send(link, i, bj, c).start()))

            @pl.when(j + d < gy)
            def _():
                bj = j + d
                arrive(i, bj, c)

                @pl.when(j > 0)
                def _():
                    send(1, i, bj, c).start()

                crossed(d, bj, c, lambda: x_links(lambda link: send(link, i, bj, c).start()))

            if d == 1 and turned:
                @pl.when(c < turned)
                def _():
                    arrive(other, j, c)

                    @pl.when(pair > j)
                    def _():
                        send(0, other, j, c).start()

                    @pl.when(pair < j)
                    def _():
                        send(1, other, j, c).start()

        each(groups, column)

        @pl.when(j - d >= 0)
        def _():
            pass

        @pl.when(j + d < gy)
        def _():
            pass

    def block_rows(body):
        body(j, True)
        for d in range(1, gy):
            @pl.when(j - d >= 0)
            def _():
                body(j - d, False)

            @pl.when(j + d < gy)
            def _():
                body(j + d, False)

    for d in range(1, gx):
        def row(bj, first, d=d):
            @pl.when(i - d >= 0)
            def _():
                def take(c):
                    arrive(i - d, bj, c)

                    @pl.when(i + 1 < gx)
                    def _():
                        send(2, i - d, bj, c).start()

                each(groups, take, turned if first else 0)
                pass

            @pl.when(i + d < gx)
            def _():
                def take(c):
                    arrive(i + d, bj, c)

                    @pl.when(i > 0)
                    def _():
                        send(3, i + d, bj, c).start()

                each(groups, take, turned if first else 0)
                pass

        block_rows(row)

    for copy in copies:
        copy.wait_send()

    def drain(bj):
        def chunk(c):
            @pl.when((bj <= j) & (j + 1 < gy))
            def _():
                send(0, i, bj, c).wait_send()

            @pl.when((bj >= j) & (j > 0))
            def _():
                send(1, i, bj, c).wait_send()

            def sideways(link):
                send(link, i, bj, c).wait_send()

            if turned:
                @pl.when((bj != pair) | (c >= turned))
                def _():
                    x_links(sideways)
            else:
                x_links(sideways)

            for d in range(1, gx):
                @pl.when((i - d >= 0) & (i + 1 < gx))
                def _():
                    send(2, i - d, bj, c).wait_send()

                @pl.when((i + d < gx) & (i > 0))
                def _():
                    send(3, i + d, bj, c).wait_send()

        each(groups, chunk)

    each(gy, drain)
    if turned:
        def drain_turned(c):
            @pl.when(pair > j)
            def _():
                send(0, other, j, c).wait_send()

            @pl.when(pair < j)
            def _():
                send(1, other, j, c).wait_send()

        each(turned, drain_turned)


def put_out(ns_in, na_in, slab_in, ns_out, na_out, slab_out, sem):
    pairs = []
    place = 0
    for first, size in RUNS:
        pairs.append((slab_in.at[pl.ds(place, size)], slab_out.at[pl.ds(first, size)]))
        place += size
    pairs += [(ns_in, ns_out), (na_in, na_out)]
    copies = [pltpu.make_async_copy(a, b, sem.at[n]) for n, (a, b) in enumerate(pairs)]
    for copy in copies:
        copy.start()
    for copy in copies:
        copy.wait()


def shards(sizes, section, base, accum):
    gx, gy, gz = sizes
    fields, planes, rows, lanes = section.shape
    groups = GROUPS
    slots = 1 if gx == 2 else 2
    n_messages = 4 * groups + 4 + 5 * slots
    any_spec = pl.BlockSpec(memory_space=pl.ANY)
    block = jax.ShapeDtypeStruct(section.shape, jnp.float32)
    slab = jax.ShapeDtypeStruct((fields, planes, gy * rows, gx * lanes), jnp.float32)
    dma = pltpu.SemaphoreType.DMA
    staged = pl.pallas_call(
        functools.partial(section_kernel, sizes, groups),
        out_shape=tuple(pltpu.VMEM(a.shape, a.dtype) for a in (block, block, slab)),
        in_specs=[pl.BlockSpec(memory_space=pltpu.HBM)] * 3,
        out_specs=(pl.BlockSpec(memory_space=pltpu.VMEM),) * 3,
        scratch_shapes=[
            pltpu.VMEM((fields, planes + 4, rows + 2 * PAD, lanes), jnp.float32),
            pltpu.VMEM((slots, planes + 4, rows + 2 * PAD, lanes), jnp.float32),
            pltpu.VMEM((1, planes, rows, lanes), jnp.float32),
            pltpu.VMEM(section.shape, jnp.float32),
            pltpu.VMEM(section.shape, jnp.float32),
            dma((2 + len(RUNS),)),
            dma((n_messages,)),
            dma((n_messages,)),
            dma((4, gx, gy, groups)),
            dma((gx, gy, groups)),
        ],
        compiler_params=pltpu.CompilerParams(collective_id=0, has_side_effects=True, vmem_limit_bytes=24 << 20),
    )(*(pltpu.with_memory_space_constraint(x, pltpu.HBM) for x in (section, base, accum)))
    return pl.pallas_call(
        put_out,
        out_shape=(block, block, slab),
        in_specs=[pl.BlockSpec(memory_space=pltpu.VMEM)] * 3,
        out_specs=(any_spec,) * 3,
        scratch_shapes=[dma((2 + len(RUNS),))],
        compiler_params=pltpu.CompilerParams(vmem_limit_bytes=8 << 20),
    )(*staged)


def solution(mesh):
    sizes = tuple(mesh.shape[name] for name in ("gx", "gy", "gz"))
    spec = P(None, "gz", "gy", "gx")
    return jax.shard_map(
        functools.partial(shards, sizes),
        mesh=mesh,
        in_specs=(spec, spec, spec),
        out_specs=(spec, spec, P(None, "gz", None, None)),
        check_vma=False,
    )
```

profile of v0, /device:TPU:0, one launch (start us, length us, event | category | flops | bytes accessed | tf_op | source)
XLA Modules:
  0.0 51.6 jit_solution(4509550920546317119)
XLA Ops:
  0.6 48.9 %shard_map.58 = (f32[25,2,16,128]{3,2,1,0:T(8,128)S(1)}, f32[25,2,16,128]{3,2,1,0:T(8,128)S(1)}, f32[25,2,64,256]{3,2,1,0:T(8,128)S(1)}) custom-call(f32[25,2,16,128]{3,2,1,0:T(8,128)} %section.1, f32[25,2,16,128]{3,2,1,0:T(8,128)} %base.1, f32[25,2,16,128]{3,2,1,0:T(8,128)} %accum.1), custom_call_target="tpu_custom_call" | custom-call | tf_op jit(solution)/shard_map/pallas_call | solution.py:648
  49.6 2.1 %shard_map.59 = (f32[25,2,16,128]{3,2,1,0:T(8,128)}, f32[25,2,16,128]{3,2,1,0:T(8,128)}, f32[25,2,64,256]{3,2,1,0:T(8,128)}) custom-call(f32[25,2,16,128]{3,2,1,0:T(8,128)S(1)} %get-tuple-element.6.ns_in, f32[25,2,16,128]{3,2,1,0:T(8,128)S(1)} %get-tuple-element.7.na_in, f32[25,2,64,256]{3,2,1,0:T(8,128)S(1)} %get-tuple-element.8.slab_in), custom_call_target="tpu_custom_call" | custom-call | tf_op jit(solution)/shard_map/pallas_call | solution.py:667
where the time goes:
time: 51.9 us; the launch traced here: 51.6 us
  Pallas kernels  51 us (98%)
  between operations  0.64 us (1%)
    pallas_call x1, Pallas kernels, shards(): pl.pallas_call(functools.partial(section_kernel, sizes, groups), out_shap...  48.9 us
    pallas_call x1, Pallas kernels, shards(): pl.pallas_call(put_out, out_shape=(block, block, slab), in_specs=[pl.Bloc...  2.05 us

commit v1 on v0

v1 whole, which is shorter than its diff:
```python
import functools

import jax
import jax.numpy as jnp
from jax import lax
from jax.experimental import pallas as pl
from jax.experimental.pallas import tpu as pltpu
from jax.sharding import PartitionSpec as P

STEP_DT = 0.25
DISSIPATE = 0.1
DRIVER_ETA = 2.0
KAPPA_ONE = 0.1
PAIR_SLOT = ((0, 1, 2), (1, 3, 4), (2, 4, 5))
PAIR_LIST = ((0, 0), (0, 1), (0, 2), (1, 1), (1, 2), (2, 2))
MESH = pl.DeviceIdType.MESH
RUNS = ((17, 4), (0, 8), (14, 3), (8, 6), (21, 4))
ORDER = tuple(first + n for first, size in RUNS for n in range(size))
PLACE = tuple(ORDER.index(field) for field in range(len(ORDER)))
MIXED = (17, 18, 19, 20, 0)
SIZES = (1, 4, 3, 3, 2, 4, 4, 4)
STAGES = len(SIZES)
FIRST = tuple(sum(SIZES[:s]) for s in range(STAGES + 1))
MIX_STAGE = 4
TURNED = 3
TURN_LAG = 6
Y_GROUPS = ((0, 1), (1, 2), (2, STAGES))
PAD = 8


def first_of(m2, m1, p1, p2):
    return (8.0 / 12.0) * (p1 - m1) - (1.0 / 12.0) * (p2 - m2)


def rates_of_plane(plane, rows, lanes, xb, tb, emit):
    lane = lax.broadcasted_iota(jnp.int32, (rows, lanes), 1)
    quad = lane & 3
    edge_one = (lane < 1) | (lane >= lanes - 1)
    edge_two = (lane < 2) | (lane >= lanes - 2)

    def cell(field, dz=0, dy=0):
        return xb[PLACE[field], plane + 2 + dz, PAD + dy : PAD + dy + rows, :]

    def strip(dz=0, dy=0):
        def side(slot):
            return tb[slot, plane + 2 + dz, PAD + dy : PAD + dy + rows, :]

        if tb.shape[0] == 1:
            return side(0)
        return jnp.where(quad < 2, side(1), side(0))

    def inner(edge):
        return jnp.where(
            quad == 1, pltpu.roll(edge, 1, 1), pltpu.roll(edge, lanes - 1, 1)
        )

    def x_line(field, value, edge, edge_in):
        turn = (lanes - 2 - 4 * field) % lanes
        two = pltpu.roll(edge, turn, 1)
        one = pltpu.roll(edge_in, turn, 1)
        m2 = jnp.where(edge_two & (lane < 64), two, pltpu.roll(value, 2, 1))
        m1 = jnp.where(edge_one & (lane < 64), one, pltpu.roll(value, 1, 1))
        p1 = jnp.where(edge_one & (lane >= 64), one, pltpu.roll(value, lanes - 1, 1))
        p2 = jnp.where(edge_two & (lane >= 64), two, pltpu.roll(value, lanes - 2, 1))
        return m2, m1, p1, p2

    def y_line(read):
        return tuple(read(0, dy) for dy in (-2, -1, 1, 2))

    def z_line(read):
        return tuple(read(dz, 0) for dz in (-2, -1, 1, 2))

    edge = strip()
    edge_in = inner(edge)

    centre, grad, curve, lap, mixed = {}, {}, {}, {}, {}
    need_lap = (0, 1, 2, 3, 4, 5, 6, 17, 18, 19, 20)
    shift = [cell(18), cell(19), cell(20)]
    advected = {}
    for field in range(len(ORDER)):
        centre[field] = cell(field)

    def differentiate(field):
        value = centre[field]
        read = functools.partial(cell, field)
        lines = [x_line(field, value, edge, edge_in), y_line(read), z_line(read)]
        near = [m1 + p1 for _, m1, p1, _ in lines]
        far = [m2 + p2 for m2, _, _, p2 in lines]
        near_sum = near[0] + near[1] + near[2]
        far_sum = far[0] + far[1] + far[2]
        smooth = far_sum - 4.0 * near_sum + 18.0 * value
        grads = [first_of(*line) for line in lines]
        grad[field] = grads
        advected[field] = (
            shift[0] * grads[0] + shift[1] * grads[1] + shift[2] * grads[2]
            - (DISSIPATE / 16.0) * smooth
        )
        if field in need_lap:
            lap[field] = (16.0 / 12.0) * near_sum - (1.0 / 12.0) * far_sum - 7.5 * value
        if field in MIXED:
            for axis in range(3):
                if field in (0, 17) or field == 18 + axis:
                    curve[field, axis] = (
                        (16.0 / 12.0) * near[axis] - (1.0 / 12.0) * far[axis] - 2.5 * value
                    )

    def mix():
        edge_y = first_of(*y_line(strip))
        edge_y_in = inner(edge_y)
        edge_z = first_of(*z_line(strip))
        edge_z_in = inner(edge_z)
        for field in MIXED:
            grads = grad[field]
            if field != 20:
                mixed[field, 0, 1] = first_of(*x_line(field, grads[1], edge_y, edge_y_in))
            if field != 19:
                mixed[field, 0, 2] = first_of(*x_line(field, grads[2], edge_z, edge_z_in))
            if field != 18:
                mixed[field, 1, 2] = first_of(
                    *(
                        first_of(*(cell(field, dz, dy) for dy in (-2, -1, 1, 2)))
                        for dz in (-2, -1, 1, 2)
                    )
                )

    def second(field, one, two):
        if one == two:
            return curve[field, one]
        return mixed[field, min(one, two), max(one, two)]

    def sym(table, one, two):
        return table[PAIR_SLOT[one][two]]

    metric = [centre[1 + k] for k in range(6)]
    traceless = [centre[8 + k] for k in range(6)]
    inverse = [
        (2.0 - metric[k]) if one == two else -metric[k]
        for k, (one, two) in enumerate(PAIR_LIST)
    ]

    def contract(left, right):
        diag = left[0] * right[0] + left[3] * right[3] + left[5] * right[5]
        off = left[1] * right[1] + left[2] * right[2] + left[4] * right[4]
        return diag + 2.0 * off

    def lie_of(table, one, two):
        total = None
        for k in range(3):
            if one == two:
                term = 2.0 * (sym(table, one, k) * grad[18 + k][one])
            else:
                term = (
                    sym(table, one, k) * grad[18 + k][two]
                    + sym(table, two, k) * grad[18 + k][one]
                )
            total = term if total is None else total + term
        return total

    def begin(stage):
        for field in ORDER[FIRST[stage] : FIRST[stage + 1]]:
            differentiate(field)

    chi, trace, lapse, theta = centre[0], centre[7], centre[17], centre[24]

    begin(0)
    emit(17, advected[17] - 2.0 * lapse * (trace - 2.0 * theta))
    yield

    begin(1)
    div = grad[18][0] + grad[19][1] + grad[20][2]
    third_div = (2.0 / 3.0) * div
    for one in range(3):
        emit(18 + one, advected[18 + one] + 0.75 * centre[21 + one])
    emit(0, advected[0] + (2.0 / 3.0) * chi * (lapse * trace) - chi * third_div)
    yield

    def metric_rate(k):
        one, two = PAIR_LIST[k]
        emit(
            1 + k,
            advected[1 + k]
            - 2.0 * lapse * traceless[k]
            + lie_of(metric, one, two)
            - metric[k] * third_div,
        )

    for stage in (2, 3):
        begin(stage)
        for field in ORDER[FIRST[stage] : FIRST[stage + 1]]:
            metric_rate(field - 1)
        yield

    begin(4)
    mix()
    over_chi = 1.0 / chi
    half_over = 0.5 * over_chi
    squares = contract(traceless, traceless)
    lapse_dd = [second(17, one, two) for one, two in PAIR_LIST]
    lapse_trace = contract(inverse, lapse_dd)
    emit(
        7,
        advected[7]
        - chi * lapse_trace
        + lapse * (squares + trace * trace * (1.0 / 3.0))
        + KAPPA_ONE * lapse * theta,
    )
    gauges = []

    def connection_rate(one):
        a_lapse = sum(sym(traceless, one, k) * grad[17][k] for k in range(3))
        a_chi = sum(sym(traceless, one, k) * grad[0][k] for k in range(3))
        g_trace = sum(sym(inverse, one, k) * grad[7][k] for k in range(3))
        b_mixed = sum(second(18 + k, one, k) for k in range(3))
        g_shift = sum(centre[14 + k] * grad[18 + one][k] for k in range(3))
        gauge = (
            -2.0 * a_lapse
            - lapse * ((4.0 / 3.0) * g_trace + 3.0 * (a_chi * over_chi))
            + lap[18 + one]
            + b_mixed * (1.0 / 3.0)
            + centre[14 + one] * third_div
            - g_shift
        )
        gauges.append(gauge)
        emit(14 + one, advected[14 + one] + gauge)

    connection_rate(0)
    yield

    begin(5)
    connection_rate(1)
    connection_rate(2)
    ricci = []
    for k, (one, two) in enumerate(PAIR_LIST):
        conf = second(0, one, two)
        if one == two:
            conf = conf + lap[0]
            grads_g = grad[14 + one][one]
        else:
            grads_g = 0.5 * (grad[14 + two][one] + grad[14 + one][two])
        ricci.append(-0.5 * lap[1 + k] + grads_g + conf * half_over)
    ricci_trace = contract(inverse, ricci)
    third_trace = (lapse * ricci_trace - lapse_trace) * (1.0 / 3.0)

    def traceless_rate(k):
        one, two = PAIR_LIST[k]
        free = lapse * ricci[k] - lapse_dd[k] - metric[k] * third_trace
        product = sum(
            sym(traceless, one, m) * sym(traceless, m, two) for m in range(3)
        )
        emit(
            8 + k,
            advected[8 + k]
            + chi * free
            + lapse * (trace * traceless[k] - 2.0 * product)
            + lie_of(traceless, one, two)
            - traceless[k] * third_div,
        )

    traceless_rate(0)
    traceless_rate(1)
    yield

    begin(6)
    for k in range(2, 6):
        traceless_rate(k)
    yield

    begin(7)
    for one in range(3):
        emit(21 + one, advected[21 + one] + gauges[one] - DRIVER_ETA * centre[21 + one])
    emit(
        24,
        advected[24]
        + 0.5 * lapse * (chi * ricci_trace + (2.0 / 3.0) * trace * trace - squares)
        - 2.0 * KAPPA_ONE * lapse * theta,
    )
    yield


def section_kernel(
    sizes, section, base, accum, ns_out, na_out, slab,
    xb, tb, tile, bb, ab, local_sem, halo_send, halo_recv,
    line_send, gather_recv,
):
    gx, gy, gz = sizes
    fields, planes, rows, lanes = section.shape
    i, j, k = (lax.axis_index(name) for name in ("gx", "gy", "gz"))

    def device(dx=0, dy=0, dz=0):
        return (
            lax.rem(i + dx + gx, gx),
            lax.rem(j + dy + gy, gy),
            lax.rem(k + dz + gz, gz),
        )

    x_steps = (1,) if gx == 2 else (1, -1)

    copies = []

    def halo(delta, src, dst):
        m = len(copies)
        copies.append(
            pltpu.make_async_remote_copy(
                src_ref=src, dst_ref=dst, send_sem=halo_send.at[m], recv_sem=halo_recv.at[m],
                device_id=device(*delta), device_id_type=MESH,
            )
        )
        return copies[-1]

    own_planes, own_rows = pl.ds(2, planes), pl.ds(PAD, rows)

    def planes_of(dz):
        if dz == 1:
            return pl.ds(planes, 2), pl.ds(0, 2)
        return pl.ds(2, 2), pl.ds(2 + planes, 2)

    def rows_of(dy):
        if dy == 1:
            return pl.ds(PAD + rows - 2, 2), pl.ds(PAD - 2, 2)
        return pl.ds(PAD, 2), pl.ds(PAD + rows, 2)

    def run_of(low, high):
        return pl.ds(FIRST[low], FIRST[high] - FIRST[low])

    def z_face(stage, dz):
        run = run_of(stage, stage + 1)
        src, dst = planes_of(dz)
        return halo((0, 0, dz), xb.at[run, src, own_rows, :], xb.at[run, dst, own_rows, :])

    def y_face(group, dy):
        run = run_of(*group)
        src, dst = rows_of(dy)
        return halo((0, dy, 0), xb.at[run, own_planes, src, :], xb.at[run, own_planes, dst, :])

    def yz_edge(dy, side):
        run = pl.ds(0, len(MIXED))
        src, dst = rows_of(dy)
        cut = pl.ds(0, 2) if side == 0 else pl.ds(2 + planes, 2)
        return halo((0, dy, 0), xb.at[run, cut, src, :], xb.at[run, cut, dst, :])

    def xy_edge(slot, dy):
        src, dst = rows_of(dy)
        return halo((0, dy, 0), tb.at[slot, own_planes, src, :], tb.at[slot, own_planes, dst, :])

    def xz_edge(slot, dz):
        src, dst = planes_of(dz)
        return halo((0, 0, dz), tb.at[slot, src, own_rows, :], tb.at[slot, dst, own_rows, :])

    z_faces = [[z_face(s, dz) for dz in (1, -1)] for s in range(STAGES)]
    y_faces = [[y_face(g, dy) for dy in (1, -1)] for g in Y_GROUPS]
    yz_edges = [yz_edge(dy, side) for dy in (1, -1) for side in (0, 1)]
    x_faces = [
        halo((dx, 0, 0), tile.at[0], tb.at[slot, own_planes, own_rows, :])
        for slot, dx in enumerate(x_steps)
    ]
    slots = range(len(x_steps))
    xy_edges = [xy_edge(slot, dy) for slot in slots for dy in (1, -1)]
    xz_edges = [xz_edge(slot, dz) for slot in slots for dz in (1, -1)]

    def start(some):
        for copy in some:
            copy.start()

    def await_recv(some):
        for copy in some:
            copy.wait_recv()

    loads = []
    place = 0
    for first, size in RUNS:
        loads.append(
            pltpu.make_async_copy(
                section.at[pl.ds(first, size)],
                xb.at[pl.ds(place, size), own_planes, own_rows, :],
                local_sem.at[2 + len(loads)],
            )
        )
        place += size
    load_base = pltpu.make_async_copy(base, bb, local_sem.at[0])
    load_accum = pltpu.make_async_copy(accum, ab, local_sem.at[1])
    partners = [(0, 0, 1), (0, 0, -1)] + [(dx, 0, 0) for dx in x_steps] + [(0, 1, 0), (0, -1, 0)]
    start(loads)
    barrier = pltpu.get_barrier_semaphore()
    for delta in partners:
        pl.semaphore_signal(barrier, inc=1, device_id=device(*delta), device_id_type=MESH)
    load_base.start()
    load_accum.start()

    lane = lax.broadcasted_iota(jnp.int32, (rows, lanes), 1)

    def pack(plane, carry):
        packed = jnp.zeros((rows, lanes), jnp.float32)
        for field in range(fields):
            value = xb[PLACE[field], plane + 2, PAD : PAD + rows, :]
            ends = jnp.where(lane < 2, value, pltpu.roll(value, 4, 1))
            if field:
                ends = pltpu.roll(ends, 4 * field, 1)
            packed = jnp.where((lane >> 2) == field, ends, packed)
        tile[0, plane] = packed
        return carry

    for load in loads:
        load.wait()
    pl.semaphore_wait(barrier, len(partners))
    start(z_faces[0] + y_faces[0] + z_faces[1] + y_faces[1])
    lax.fori_loop(0, planes, pack, 0)
    start(x_faces + z_faces[2] + y_faces[2])
    load_base.wait()
    load_accum.wait()

    own_y = pl.ds(pl.multiple_of(j * rows, rows), rows)
    own_x = pl.ds(pl.multiple_of(i * lanes, lanes), lanes)
    paired = gx == 2 and gy % 2 == 0
    turned = TURNED if paired else 0
    kept = STAGES - turned
    pair = j + 1 - 2 * lax.rem(j, 2)
    other = 1 - i
    towards = ((0, 1), (0, -1), (1, 0), (-1, 0))
    BULK, BULK_TURNED = STAGES, STAGES + 1

    def piece(bi, bj, low, high):
        return slab.at[
            run_of(low, high),
            :,
            pl.ds(pl.multiple_of(bj * rows, rows), rows),
            pl.ds(pl.multiple_of(bi * lanes, lanes), lanes),
        ]

    def line(link, bi, bj, low, high, slot):
        dx, dy = towards[link]
        part = piece(bi, bj, low, high)
        return pltpu.make_async_remote_copy(
            src_ref=part,
            dst_ref=part,
            send_sem=line_send.at[link, bi, bj, 0 if low < kept else 1],
            recv_sem=gather_recv.at[bi, bj, slot],
            device_id=device(dx, dy, 0),
            device_id_type=MESH,
        )

    def send(link, bi, bj, c, own=False):
        slot = c
        if paired and link == 2:
            if c < kept:
                slot = BULK
            elif not own:
                slot = BULK_TURNED
        line(link, bi, bj, c, c + 1, slot).start()

    def arrive(bi, bj, c):
        line(0, bi, bj, c, c + 1, c).wait_recv()

    def x_links(body):
        if paired:
            body(2)
            return

        @pl.when(i + 1 < gx)
        def _():
            body(2)

        @pl.when(i > 0)
        def _():
            body(3)

    def send_own(c):
        @pl.when(j + 1 < gy)
        def _():
            send(0, i, j, c)

        @pl.when(j > 0)
        def _():
            send(1, i, j, c)

        x_links(lambda link: send(link, i, j, c, True))

    def crossed(d, bj, c):
        def cross():
            x_links(lambda link: send(link, i, bj, c))

        if d == 1 and c >= kept:
            pl.when(bj != pair)(cross)
        else:
            cross()

    def pass_on(d, c):
        @pl.when(j - d >= 0)
        def _():
            bj = j - d
            arrive(i, bj, c)

            @pl.when(j + 1 < gy)
            def _():
                send(0, i, bj, c)

            crossed(d, bj, c)

        @pl.when(j + d < gy)
        def _():
            bj = j + d
            arrive(i, bj, c)

            @pl.when(j > 0)
            def _():
                send(1, i, bj, c)

            crossed(d, bj, c)

    def turn(c):
        arrive(other, j, c)

        @pl.when(pair > j)
        def _():
            line(0, other, j, c, c + 1, BULK_TURNED).start()

        @pl.when(pair < j)
        def _():
            line(1, other, j, c, c + 1, BULK_TURNED).start()

    def emit_at(plane):
        def emit(field, rate):
            moved = bb[field, plane] + (0.5 * STEP_DT) * rate
            slab[PLACE[field], plane, own_y, own_x] = moved
            ns_out[field, plane] = moved
            na_out[field, plane] = ab[field, plane] + (STEP_DT / 3.0) * rate

        return emit

    await_recv(x_faces)
    start(xz_edges + xy_edges)
    for s in range(3, STAGES):
        start(z_faces[s])
    await_recv(z_faces[0])
    work = [
        rates_of_plane(plane, rows, lanes, xb, tb, emit_at(plane))
        for plane in range(planes)
    ]

    def own_stage(s):
        if s:
            await_recv(z_faces[s])
        if s == 1:
            start(yz_edges)
        if s < len(Y_GROUPS):
            await_recv(y_faces[s])
        if s == MIX_STAGE:
            await_recv(xy_edges + xz_edges + yz_edges)
        for part in work:
            next(part)
        send_own(s)

    LAG = tuple(1 + 2 * d for d in range(gy))
    for v in range(STAGES + max(LAG)):
        if v < STAGES:
            own_stage(v)
        for d in range(1, gy):
            if 0 <= v - LAG[d] < STAGES:
                pass_on(d, v - LAG[d])
        if kept <= v - TURN_LAG < STAGES:
            turn(v - TURN_LAG)

    def over_blocks(body):
        lax.fori_loop(0, gy, lambda bj, carry: (body(bj), carry)[1], 0)

    for copy in copies:
        copy.wait_send()

    if paired:
        def last(bj):
            line(2, other, bj, 0, kept, BULK).wait_recv()
            if turned:
                @pl.when(bj != j)
                def _():
                    line(2, other, bj, kept, STAGES, BULK_TURNED).wait_recv()

        over_blocks(last)
    else:
        for d in range(1, gx):
            def row(bj, d=d):
                @pl.when(i - d >= 0)
                def _():
                    for c in range(STAGES):
                        arrive(i - d, bj, c)

                        @pl.when(i + 1 < gx)
                        def _():
                            send(2, i - d, bj, c)

                @pl.when(i + d < gx)
                def _():
                    for c in range(STAGES):
                        arrive(i + d, bj, c)

                        @pl.when(i > 0)
                        def _():
                            send(3, i + d, bj, c)

            over_blocks(row)

    def drain(bj):
        def sent(link, bi, low=0, high=STAGES):
            if low < kept:
                line(link, bi, bj, low, min(high, kept), 0).wait_send()
            if high > kept:
                line(link, bi, bj, kept, high, 0).wait_send()

        @pl.when((bj <= j) & (j + 1 < gy))
        def _():
            sent(0, i)

        @pl.when((bj >= j) & (j > 0))
        def _():
            sent(1, i)

        if paired:
            sent(2, i, 0, kept)
            if turned:
                @pl.when(bj != pair)
                def _():
                    sent(2, i, kept, STAGES)
        else:
            x_links(lambda link: sent(link, i))
            for d in range(1, gx):
                @pl.when((i - d >= 0) & (i + 1 < gx))
                def _():
                    sent(2, i - d)

                @pl.when((i + d < gx) & (i > 0))
                def _():
                    sent(3, i + d)

    over_blocks(drain)
    if turned:
        @pl.when(pair > j)
        def _():
            line(0, other, j, kept, STAGES, 0).wait_send()

        @pl.when(pair < j)
        def _():
            line(1, other, j, kept, STAGES, 0).wait_send()


def put_out(ns_in, na_in, slab_in, ns_out, na_out, slab_out, sem):
    pairs = []
    place = 0
    for first, size in RUNS:
        pairs.append((slab_in.at[pl.ds(place, size)], slab_out.at[pl.ds(first, size)]))
        place += size
    pairs += [(ns_in, ns_out), (na_in, na_out)]
    copies = [pltpu.make_async_copy(a, b, sem.at[n]) for n, (a, b) in enumerate(pairs)]
    for copy in copies:
        copy.start()
    for copy in copies:
        copy.wait()


def shards(sizes, section, base, accum):
    gx, gy, gz = sizes
    fields, planes, rows, lanes = section.shape
    slots = 1 if gx == 2 else 2
    n_messages = 2 * STAGES + 2 * len(Y_GROUPS) + 4 + 5 * slots
    any_spec = pl.BlockSpec(memory_space=pl.ANY)
    block = jax.ShapeDtypeStruct(section.shape, jnp.float32)
    slab = jax.ShapeDtypeStruct((fields, planes, gy * rows, gx * lanes), jnp.float32)
    dma = pltpu.SemaphoreType.DMA
    staged = pl.pallas_call(
        functools.partial(section_kernel, sizes),
        out_shape=tuple(pltpu.VMEM(a.shape, a.dtype) for a in (block, block, slab)),
        in_specs=[pl.BlockSpec(memory_space=pltpu.HBM)] * 3,
        out_specs=(pl.BlockSpec(memory_space=pltpu.VMEM),) * 3,
        scratch_shapes=[
            pltpu.VMEM((fields, planes + 4, rows + 2 * PAD, lanes), jnp.float32),
            pltpu.VMEM((slots, planes + 4, rows + 2 * PAD, lanes), jnp.float32),
            pltpu.VMEM((1, planes, rows, lanes), jnp.float32),
            pltpu.VMEM(section.shape, jnp.float32),
            pltpu.VMEM(section.shape, jnp.float32),
            dma((2 + len(RUNS),)),
            dma((n_messages,)),
            dma((n_messages,)),
            dma((4, gx, gy, 2)),
            dma((gx, gy, STAGES + 2)),
        ],
        compiler_params=pltpu.CompilerParams(collective_id=0, has_side_effects=True, vmem_limit_bytes=24 << 20),
    )(*(pltpu.with_memory_space_constraint(x, pltpu.HBM) for x in (section, base, accum)))
    return pl.pallas_call(
        put_out,
        out_shape=(block, block, slab),
        in_specs=[pl.BlockSpec(memory_space=pltpu.VMEM)] * 3,
        out_specs=(any_spec,) * 3,
        scratch_shapes=[dma((2 + len(RUNS),))],
        compiler_params=pltpu.CompilerParams(vmem_limit_bytes=8 << 20),
    )(*staged)


def solution(mesh):
    sizes = tuple(mesh.shape[name] for name in ("gx", "gy", "gz"))
    spec = P(None, "gz", "gy", "gx")
    return jax.shard_map(
        functools.partial(shards, sizes),
        mesh=mesh,
        in_specs=(spec, spec, spec),
        out_specs=(spec, spec, P(None, "gz", None, None)),
        check_vma=False,
    )
```

time: 51.9 us -> 47.3 us (0.911)
  Pallas kernels: 51 us -> 46.5 us
    pallas_call x1, Pallas kernels: 48.9 us -> 44.5 us  [shards(): pl.pallas_call(functools.partial(section_kernel, sizes), out_shape=tuple(...]
where the time goes in v1:
time: 47.3 us; the launch traced here: 47.1 us
  Pallas kernels  46.5 us (98%)
  between operations  0.64 us (1%)
    pallas_call x1, Pallas kernels, shards(): pl.pallas_call(functools.partial(section_kernel, sizes), out_shape=tuple(...  44.5 us
    pallas_call x1, Pallas kernels, shards(): pl.pallas_call(put_out, out_shape=(block, block, slab), in_specs=[pl.Bloc...  2.03 us

profile of v1, /device:TPU:0, one launch (start us, length us, event | category | flops | bytes accessed | tf_op | source)
XLA Modules:
  0.0 47.1 jit_solution(17172476283085421629)
XLA Ops:
  0.6 44.5 %shard_map.58 = (f32[25,2,16,128]{3,2,1,0:T(8,128)S(1)}, f32[25,2,16,128]{3,2,1,0:T(8,128)S(1)}, f32[25,2,64,256]{3,2,1,0:T(8,128)S(1)}) custom-call(f32[25,2,16,128]{3,2,1,0:T(8,128)} %section.1, f32[25,2,16,128]{3,2,1,0:T(8,128)} %base.1, f32[25,2,16,128]{3,2,1,0:T(8,128)} %accum.1), custom_call_target="tpu_custom_call" | custom-call | tf_op jit(solution)/shard_map/pallas_call | solution.py:666
  45.1 2.0 %shard_map.59 = (f32[25,2,16,128]{3,2,1,0:T(8,128)}, f32[25,2,16,128]{3,2,1,0:T(8,128)}, f32[25,2,64,256]{3,2,1,0:T(8,128)}) custom-call(f32[25,2,16,128]{3,2,1,0:T(8,128)S(1)} %get-tuple-element.6.ns_in, f32[25,2,16,128]{3,2,1,0:T(8,128)S(1)} %get-tuple-element.7.na_in, f32[25,2,64,256]{3,2,1,0:T(8,128)S(1)} %get-tuple-element.8.slab_in), custom_call_target="tpu_custom_call" | custom-call | tf_op jit(solution)/shard_map/pallas_call | solution.py:685

commit v2 on v1

--- a/solution.py
+++ b/solution.py
@@ -47,7 +47,12 @@
 
         if tb.shape[0] == 1:
             return side(0)
-        return jnp.where(quad < 2, side(1), side(0))
+        return jnp.where(quad < 2, side(0), side(1))
+
+    def facing(edge):
+        return jnp.where(
+            quad < 2, pltpu.roll(edge, lanes - 2, 1), pltpu.roll(edge, 2, 1)
+        )
 
     def inner(edge):
         return jnp.where(
@@ -70,7 +75,7 @@
     def z_line(read):
         return tuple(read(dz, 0) for dz in (-2, -1, 1, 2))
 
-    edge = strip()
+    edge = facing(strip())
     edge_in = inner(edge)
 
     centre, grad, curve, lap, mixed = {}, {}, {}, {}, {}
@@ -105,9 +110,9 @@
                     )
 
     def mix():
-        edge_y = first_of(*y_line(strip))
+        edge_y = facing(first_of(*y_line(strip)))
         edge_y_in = inner(edge_y)
-        edge_z = first_of(*z_line(strip))
+        edge_z = facing(first_of(*z_line(strip)))
         edge_z_in = inner(edge_z)
         for field in MIXED:
             grads = grad[field]
@@ -295,19 +300,30 @@
 
     x_steps = (1,) if gx == 2 else (1, -1)
 
-    copies = []
-
-    def halo(delta, src, dst):
-        m = len(copies)
-        copies.append(
-            pltpu.make_async_remote_copy(
-                src_ref=src, dst_ref=dst, send_sem=halo_send.at[m], recv_sem=halo_recv.at[m],
-                device_id=device(*delta), device_id_type=MESH,
-            )
-        )
-        return copies[-1]
+    def landed(sem, ref):
+        pltpu.make_async_remote_copy(
+            src_ref=ref, dst_ref=ref, send_sem=sem, recv_sem=sem,
+            device_id=device(0, 1, 0), device_id_type=MESH,
+        ).wait_recv()
+
+    def left(sem, ref):
+        pltpu.make_async_remote_copy(
+            src_ref=ref, dst_ref=ref, send_sem=sem, recv_sem=sem,
+            device_id=device(0, 1, 0), device_id_type=MESH,
+        ).wait_send()
 
     own_planes, own_rows = pl.ds(2, planes), pl.ds(PAD, rows)
+    SENT = dict(z=0, y=1, yz=2, x=3, xy=4, xz=5)
+    GOT_Z, GOT_Y = 0, STAGES
+    GOT_YZ = STAGES + len(Y_GROUPS)
+    GOT_X, GOT_XY, GOT_XZ = GOT_YZ + 1, GOT_YZ + 2, GOT_YZ + 3
+
+    def halo(delta, kind, got, src, dst):
+        return pltpu.make_async_remote_copy(
+            src_ref=src, dst_ref=dst,
+            send_sem=halo_send.at[SENT[kind]], recv_sem=halo_recv.at[got],
+            device_id=device(*delta), device_id_type=MESH,
+        )
 
     def planes_of(dz):
         if dz == 1:
@@ -325,45 +341,77 @@
     def z_face(stage, dz):
         run = run_of(stage, stage + 1)
         src, dst = planes_of(dz)
-        return halo((0, 0, dz), xb.at[run, src, own_rows, :], xb.at[run, dst, own_rows, :])
+        return halo(
+            (0, 0, dz), "z", GOT_Z + stage,
+            xb.at[run, src, own_rows, :], xb.at[run, dst, own_rows, :],
+        )
 
     def y_face(group, dy):
-        run = run_of(*group)
+        run = run_of(*Y_GROUPS[group])
         src, dst = rows_of(dy)
-        return halo((0, dy, 0), xb.at[run, own_planes, src, :], xb.at[run, own_planes, dst, :])
+        return halo(
+            (0, dy, 0), "y", GOT_Y + group,
+            xb.at[run, own_planes, src, :], xb.at[run, own_planes, dst, :],
+        )
 
     def yz_edge(dy, side):
         run = pl.ds(0, len(MIXED))
         src, dst = rows_of(dy)
         cut = pl.ds(0, 2) if side == 0 else pl.ds(2 + planes, 2)
-        return halo((0, dy, 0), xb.at[run, cut, src, :], xb.at[run, cut, dst, :])
+        return halo((0, dy, 0), "yz", GOT_YZ, xb.at[run, cut, src, :], xb.at[run, cut, dst, :])
 
     def xy_edge(slot, dy):
         src, dst = rows_of(dy)
-        return halo((0, dy, 0), tb.at[slot, own_planes, src, :], tb.at[slot, own_planes, dst, :])
+        return halo(
+            (0, dy, 0), "xy", GOT_XY,
+            tb.at[slot, own_planes, src, :], tb.at[slot, own_planes, dst, :],
+        )
 
     def xz_edge(slot, dz):
         src, dst = planes_of(dz)
-        return halo((0, 0, dz), tb.at[slot, src, own_rows, :], tb.at[slot, dst, own_rows, :])
-
-    z_faces = [[z_face(s, dz) for dz in (1, -1)] for s in range(STAGES)]
-    y_faces = [[y_face(g, dy) for dy in (1, -1)] for g in Y_GROUPS]
-    yz_edges = [yz_edge(dy, side) for dy in (1, -1) for side in (0, 1)]
+        return halo(
+            (0, 0, dz), "xz", GOT_XZ,
+            tb.at[slot, src, own_rows, :], tb.at[slot, dst, own_rows, :],
+        )
+
+    steps, slots = (1, -1), range(len(x_steps))
+    z_faces = [[z_face(s, dz) for dz in steps] for s in range(STAGES)]
+    y_faces = [[y_face(g, dy) for dy in steps] for g in range(len(Y_GROUPS))]
+    yz_edges = [yz_edge(dy, side) for dy in steps for side in (0, 1)]
     x_faces = [
-        halo((dx, 0, 0), tile.at[0], tb.at[slot, own_planes, own_rows, :])
+        halo((dx, 0, 0), "x", GOT_X, tile.at[0], tb.at[slot, own_planes, own_rows, :])
         for slot, dx in enumerate(x_steps)
     ]
-    slots = range(len(x_steps))
-    xy_edges = [xy_edge(slot, dy) for slot in slots for dy in (1, -1)]
-    xz_edges = [xz_edge(slot, dz) for slot in slots for dz in (1, -1)]
+    xy_edges = [xy_edge(slot, dy) for slot in slots for dy in steps]
+    xz_edges = [xz_edge(slot, dz) for slot in slots for dz in steps]
+
+    def z_landed(s):
+        landed(halo_recv.at[GOT_Z + s], xb.at[run_of(s, s + 1), pl.ds(0, 4), own_rows, :])
+
+    def y_landed(g):
+        landed(halo_recv.at[GOT_Y + g], xb.at[run_of(*Y_GROUPS[g]), own_planes, pl.ds(0, 4), :])
+
+    every = pl.ds(0, len(x_steps))
+
+    def x_landed():
+        landed(halo_recv.at[GOT_X], tb.at[every, own_planes, own_rows, :])
+
+    def edges_landed():
+        landed(halo_recv.at[GOT_YZ], xb.at[pl.ds(0, len(MIXED)), pl.ds(0, 4), pl.ds(0, 4), :])
+        landed(halo_recv.at[GOT_XY], tb.at[every, own_planes, pl.ds(0, 4), :])
+        landed(halo_recv.at[GOT_XZ], tb.at[every, pl.ds(0, 4), own_rows, :])
+
+    def halos_left():
+        left(halo_send.at[SENT["z"]], slab.at[:, pl.ds(0, 2), pl.ds(0, 2 * rows), pl.ds(0, lanes)])
+        left(halo_send.at[SENT["y"]], xb.at[:, own_planes, pl.ds(0, 4), :])
+        left(halo_send.at[SENT["yz"]], xb.at[pl.ds(0, len(MIXED)), pl.ds(0, 4), pl.ds(0, 4), :])
+        left(halo_send.at[SENT["x"]], tb.at[every, own_planes, own_rows, :])
+        left(halo_send.at[SENT["xy"]], tb.at[every, own_planes, pl.ds(0, 4), :])
+        left(halo_send.at[SENT["xz"]], tb.at[every, pl.ds(0, 4), own_rows, :])
 
     def start(some):
         for copy in some:
             copy.start()
-
-    def await_recv(some):
-        for copy in some:
-            copy.wait_recv()
 
     loads = []
     place = 0
@@ -372,12 +420,12 @@
             pltpu.make_async_copy(
                 section.at[pl.ds(first, size)],
                 xb.at[pl.ds(place, size), own_planes, own_rows, :],
-                local_sem.at[2 + len(loads)],
+                local_sem.at[0],
             )
         )
         place += size
-    load_base = pltpu.make_async_copy(base, bb, local_sem.at[0])
-    load_accum = pltpu.make_async_copy(accum, ab, local_sem.at[1])
+    load_base = pltpu.make_async_copy(base, bb, local_sem.at[1])
+    load_accum = pltpu.make_async_copy(accum, ab, local_sem.at[2])
     partners = [(0, 0, 1), (0, 0, -1)] + [(dx, 0, 0) for dx in x_steps] + [(0, 1, 0), (0, -1, 0)]
     start(loads)
     barrier = pltpu.get_barrier_semaphore()
@@ -388,23 +436,18 @@
 
     lane = lax.broadcasted_iota(jnp.int32, (rows, lanes), 1)
 
-    def pack(plane, carry):
+    own_cells = xb.at[:, own_planes, own_rows, :]
+    pltpu.make_async_copy(own_cells, own_cells, local_sem.at[0]).wait()
+    for plane in range(planes):
         packed = jnp.zeros((rows, lanes), jnp.float32)
         for field in range(fields):
             value = xb[PLACE[field], plane + 2, PAD : PAD + rows, :]
-            ends = jnp.where(lane < 2, value, pltpu.roll(value, 4, 1))
-            if field:
-                ends = pltpu.roll(ends, 4 * field, 1)
+            ends = pltpu.roll(value, (4 * field + 2) % lanes, 1)
             packed = jnp.where((lane >> 2) == field, ends, packed)
         tile[0, plane] = packed
-        return carry
-
-    for load in loads:
-        load.wait()
     pl.semaphore_wait(barrier, len(partners))
-    start(z_faces[0] + y_faces[0] + z_faces[1] + y_faces[1])
-    lax.fori_loop(0, planes, pack, 0)
-    start(x_faces + z_faces[2] + y_faces[2])
+    start(z_faces[0] + y_faces[0] + x_faces)
+    start(z_faces[1] + y_faces[1] + z_faces[2] + y_faces[2] + z_faces[3])
     load_base.wait()
     load_accum.wait()
 
@@ -416,7 +459,8 @@
     pair = j + 1 - 2 * lax.rem(j, 2)
     other = 1 - i
     towards = ((0, 1), (0, -1), (1, 0), (-1, 0))
-    BULK, BULK_TURNED = STAGES, STAGES + 1
+    TURN, BULK, BULK_TURNED, PAIR_TURNED = (gy * STAGES + n for n in (0, turned, turned + 1, turned + 2))
+    SENT_PAIR, SENT_TURNED = 4, 5
 
     def piece(bi, bj, low, high):
         return slab.at[
@@ -426,42 +470,50 @@
             pl.ds(pl.multiple_of(bi * lanes, lanes), lanes),
         ]
 
-    def line(link, bi, bj, low, high, slot):
+    def line(link, bi, bj, c, sent, got):
         dx, dy = towards[link]
-        part = piece(bi, bj, low, high)
-        return pltpu.make_async_remote_copy(
+        part = piece(bi, bj, c, c + 1)
+        pltpu.make_async_remote_copy(
             src_ref=part,
             dst_ref=part,
-            send_sem=line_send.at[link, bi, bj, 0 if low < kept else 1],
-            recv_sem=gather_recv.at[bi, bj, slot],
+            send_sem=line_send.at[sent],
+            recv_sem=gather_recv.at[got],
             device_id=device(dx, dy, 0),
             device_id_type=MESH,
-        )
-
-    def send(link, bi, bj, c, own=False):
-        slot = c
-        if paired and link == 2:
-            if c < kept:
-                slot = BULK
-            elif not own:
-                slot = BULK_TURNED
-        line(link, bi, bj, c, c + 1, slot).start()
+        ).start()
+
+    def number(bi, bj, c):
+        return (bj if paired else bi * gy + bj) * STAGES + c
+
+    def send(link, bi, bj, c):
+        line(link, bi, bj, c, link, number(bi, bj, c))
 
     def arrive(bi, bj, c):
-        line(0, bi, bj, c, c + 1, c).wait_recv()
+        landed(gather_recv.at[number(bi, bj, c)], piece(bi, bj, c, c + 1))
 
     def x_links(body):
-        if paired:
+        @pl.when(i + 1 < gx)
+        def _():
             body(2)
-            return
-
-        @pl.when(i + 1 < gx)
-        def _():
-            body(2)
 
         @pl.when(i > 0)
         def _():
             body(3)
+
+    def cross(bj, c, distance):
+        if not paired:
+            x_links(lambda link: send(link, i, bj, c))
+        elif c < kept:
+            if distance == 1:
+                line(2, i, bj, c, jnp.where(bj == pair, SENT_PAIR, 2), BULK)
+            else:
+                line(2, i, bj, c, 2, BULK)
+        elif distance == 0:
+            line(2, i, bj, c, 2, TURN + c - kept)
+        elif distance == 1:
+            pl.when(bj != pair)(lambda: line(2, i, bj, c, 2, BULK_TURNED))
+        else:
+            line(2, i, bj, c, 2, BULK_TURNED)
 
     def send_own(c):
         @pl.when(j + 1 < gy)
@@ -472,16 +524,7 @@
         def _():
             send(1, i, j, c)
 
-        x_links(lambda link: send(link, i, j, c, True))
-
-    def crossed(d, bj, c):
-        def cross():
-            x_links(lambda link: send(link, i, bj, c))
-
-        if d == 1 and c >= kept:
-            pl.when(bj != pair)(cross)
-        else:
-            cross()
+        cross(j, c, 0)
 
     def pass_on(d, c):
         @pl.when(j - d >= 0)
@@ -493,7 +536,7 @@
             def _():
                 send(0, i, bj, c)
 
-            crossed(d, bj, c)
+            cross(bj, c, d)
 
         @pl.when(j + d < gy)
         def _():
@@ -504,18 +547,18 @@
             def _():
                 send(1, i, bj, c)
 
-            crossed(d, bj, c)
+            cross(bj, c, d)
 
     def turn(c):
-        arrive(other, j, c)
+        landed(gather_recv.at[TURN + c - kept], piece(other, j, c, c + 1))
 
         @pl.when(pair > j)
         def _():
-            line(0, other, j, c, c + 1, BULK_TURNED).start()
+            line(0, other, j, c, SENT_TURNED, PAIR_TURNED)
 
         @pl.when(pair < j)
         def _():
-            line(1, other, j, c, c + 1, BULK_TURNED).start()
+            line(1, other, j, c, SENT_TURNED, PAIR_TURNED)
 
     def emit_at(plane):
         def emit(field, rate):
@@ -526,11 +569,11 @@
 
         return emit
 
-    await_recv(x_faces)
+    x_landed()
     start(xz_edges + xy_edges)
-    for s in range(3, STAGES):
+    for s in range(4, STAGES):
         start(z_faces[s])
-    await_recv(z_faces[0])
+    z_landed(0)
     work = [
         rates_of_plane(plane, rows, lanes, xb, tb, emit_at(plane))
         for plane in range(planes)
@@ -538,13 +581,13 @@
 
     def own_stage(s):
         if s:
-            await_recv(z_faces[s])
+            z_landed(s)
         if s == 1:
             start(yz_edges)
         if s < len(Y_GROUPS):
-            await_recv(y_faces[s])
+            y_landed(s)
         if s == MIX_STAGE:
-            await_recv(xy_edges + xz_edges + yz_edges)
+            edges_landed()
         for part in work:
             next(part)
         send_own(s)
@@ -559,24 +602,20 @@
         if kept <= v - TURN_LAG < STAGES:
             turn(v - TURN_LAG)
 
-    def over_blocks(body):
-        lax.fori_loop(0, gy, lambda bj, carry: (body(bj), carry)[1], 0)
-
-    for copy in copies:
-        copy.wait_send()
+    halos_left()
+
+    def whole(n_rows, n_lanes, low=0, high=STAGES):
+        return slab.at[run_of(low, high), :, pl.ds(0, n_rows), pl.ds(0, n_lanes)]
 
     if paired:
-        def last(bj):
-            line(2, other, bj, 0, kept, BULK).wait_recv()
-            if turned:
-                @pl.when(bj != j)
-                def _():
-                    line(2, other, bj, kept, STAGES, BULK_TURNED).wait_recv()
-
-        over_blocks(last)
+        if turned:
+            landed(gather_recv.at[PAIR_TURNED], whole(rows, lanes, kept))
+        landed(gather_recv.at[BULK], whole(gy * rows, lanes, 0, kept))
+        if turned and gy > 2:
+            landed(gather_recv.at[BULK_TURNED], whole((gy - 2) * rows, lanes, kept))
     else:
         for d in range(1, gx):
-            def row(bj, d=d):
+            def row(bj, carry, d=d):
                 @pl.when(i - d >= 0)
                 def _():
                     for c in range(STAGES):
@@ -595,70 +634,54 @@
                         def _():
                             send(3, i + d, bj, c)
 
-            over_blocks(row)
-
-    def drain(bj):
-        def sent(link, bi, low=0, high=STAGES):
-            if low < kept:
-                line(link, bi, bj, low, min(high, kept), 0).wait_send()
-            if high > kept:
-                line(link, bi, bj, kept, high, 0).wait_send()
-
-        @pl.when((bj <= j) & (j + 1 < gy))
-        def _():
-            sent(0, i)
-
-        @pl.when((bj >= j) & (j > 0))
-        def _():
-            sent(1, i)
-
-        if paired:
-            sent(2, i, 0, kept)
-            if turned:
-                @pl.when(bj != pair)
-                def _():
-                    sent(2, i, kept, STAGES)
-        else:
-            x_links(lambda link: sent(link, i))
-            for d in range(1, gx):
-                @pl.when((i - d >= 0) & (i + 1 < gx))
-                def _():
-                    sent(2, i - d)
-
-                @pl.when((i + d < gx) & (i > 0))
-                def _():
-                    sent(3, i + d)
-
-    over_blocks(drain)
-    if turned:
-        @pl.when(pair > j)
-        def _():
-            line(0, other, j, kept, STAGES, 0).wait_send()
-
-        @pl.when(pair < j)
-        def _():
-            line(1, other, j, kept, STAGES, 0).wait_send()
+                return carry
+
+            lax.fori_loop(0, gy, row, 0)
+
+    for n in range(1, gy):
+        @pl.when(j == n - 1)
+        def _():
+            left(line_send.at[0], whole(n * rows, lanes))
+
+        @pl.when(j == gy - n)
+        def _():
+            left(line_send.at[1], whole(n * rows, lanes))
+
+    if paired:
+        left(line_send.at[2], whole((gy - 1) * rows, lanes))
+        left(line_send.at[SENT_PAIR], whole(rows, lanes, 0, kept))
+        if turned:
+            left(line_send.at[SENT_TURNED], whole(rows, lanes, kept))
+    else:
+        for n in range(1, gx):
+            @pl.when(i == n - 1)
+            def _():
+                left(line_send.at[2], whole(gy * rows, n * lanes))
+
+            @pl.when(i == gx - n)
+            def _():
+                left(line_send.at[3], whole(gy * rows, n * lanes))
 
 
 def put_out(ns_in, na_in, slab_in, ns_out, na_out, slab_out, sem):
-    pairs = []
     place = 0
     for first, size in RUNS:
-        pairs.append((slab_in.at[pl.ds(place, size)], slab_out.at[pl.ds(first, size)]))
+        pltpu.make_async_copy(
+            slab_in.at[pl.ds(place, size)], slab_out.at[pl.ds(first, size)], sem.at[0]
+        ).start()
         place += size
-    pairs += [(ns_in, ns_out), (na_in, na_out)]
-    copies = [pltpu.make_async_copy(a, b, sem.at[n]) for n, (a, b) in enumerate(pairs)]
-    for copy in copies:
-        copy.start()
-    for copy in copies:
-        copy.wait()
+    pltpu.make_async_copy(ns_in, ns_out, sem.at[1]).start()
+    pltpu.make_async_copy(na_in, na_out, sem.at[2]).start()
+    pltpu.make_async_copy(slab_in, slab_out, sem.at[0]).wait()
+    pltpu.make_async_copy(ns_in, ns_out, sem.at[1]).wait()
+    pltpu.make_async_copy(na_in, na_out, sem.at[2]).wait()
 
 
 def shards(sizes, section, base, accum):
     gx, gy, gz = sizes
     fields, planes, rows, lanes = section.shape
     slots = 1 if gx == 2 else 2
-    n_messages = 2 * STAGES + 2 * len(Y_GROUPS) + 4 + 5 * slots
+    arrivals = gy * STAGES + TURNED + 3 if gx == 2 and gy % 2 == 0 else gx * gy * STAGES
     any_spec = pl.BlockSpec(memory_space=pl.ANY)
     block = jax.ShapeDtypeStruct(section.shape, jnp.float32)
     slab = jax.ShapeDtypeStruct((fields, planes, gy * rows, gx * lanes), jnp.float32)
@@ -674,11 +697,11 @@
             pltpu.VMEM((1, planes, rows, lanes), jnp.float32),
             pltpu.VMEM(section.shape, jnp.float32),
             pltpu.VMEM(section.shape, jnp.float32),
-            dma((2 + len(RUNS),)),
-            dma((n_messages,)),
-            dma((n_messages,)),
-            dma((4, gx, gy, 2)),
-            dma((gx, gy, STAGES + 2)),
+            dma((3,)),
+            dma((6,)),
+            dma((STAGES + len(Y_GROUPS) + 4,)),
+            dma((6,)),
+            dma((arrivals,)),
         ],
         compiler_params=pltpu.CompilerParams(collective_id=0, has_side_effects=True, vmem_limit_bytes=24 << 20),
     )(*(pltpu.with_memory_space_constraint(x, pltpu.HBM) for x in (section, base, accum)))
@@ -687,7 +710,7 @@
         out_shape=(block, block, slab),
         in_specs=[pl.BlockSpec(memory_space=pltpu.VMEM)] * 3,
         out_specs=(any_spec,) * 3,
-        scratch_shapes=[dma((2 + len(RUNS),))],
+        scratch_shapes=[dma((3,))],
         compiler_params=pltpu.CompilerParams(vmem_limit_bytes=8 << 20),
     )(*staged)
 

time: 47.3 us -> 46.3 us (0.979)
  Pallas kernels: 46.5 us -> 45.5 us
    pallas_call x1, Pallas kernels: 44.5 us -> 43.5 us  [shards(): pl.pallas_call(functools.partial(section_kernel, sizes), out_shape=tuple(...]
where the time goes in v2:
time: 46.3 us; the launch traced here: 46.1 us
  Pallas kernels  45.5 us (98%)
  between operations  0.64 us (1%)
    pallas_call x1, Pallas kernels, shards(): pl.pallas_call(functools.partial(section_kernel, sizes), out_shape=tuple(...  43.5 us
    pallas_call x1, Pallas kernels, shards(): pl.pallas_call(put_out, out_shape=(block, block, slab), in_specs=[pl.Bloc...  1.99 us

profile of v2, /device:TPU:0, one launch (start us, length us, event | category | flops | bytes accessed | tf_op | source)
XLA Modules:
  0.0 46.1 jit_solution(8494635494202626833)
XLA Ops:
  0.6 43.5 %shard_map.58 = (f32[25,2,16,128]{3,2,1,0:T(8,128)S(1)}, f32[25,2,16,128]{3,2,1,0:T(8,128)S(1)}, f32[25,2,64,256]{3,2,1,0:T(8,128)S(1)}) custom-call(f32[25,2,16,128]{3,2,1,0:T(8,128)} %section.1, f32[25,2,16,128]{3,2,1,0:T(8,128)} %base.1, f32[25,2,16,128]{3,2,1,0:T(8,128)} %accum.1), custom_call_target="tpu_custom_call" | custom-call | tf_op jit(solution)/shard_map/pallas_call | solution.py:689
  44.1 2.0 %shard_map.59 = (f32[25,2,16,128]{3,2,1,0:T(8,128)}, f32[25,2,16,128]{3,2,1,0:T(8,128)}, f32[25,2,64,256]{3,2,1,0:T(8,128)}) custom-call(f32[25,2,16,128]{3,2,1,0:T(8,128)S(1)} %get-tuple-element.6.ns_in, f32[25,2,16,128]{3,2,1,0:T(8,128)S(1)} %get-tuple-element.7.na_in, f32[25,2,64,256]{3,2,1,0:T(8,128)S(1)} %get-tuple-element.8.slab_in), custom_call_target="tpu_custom_call" | custom-call | tf_op jit(solution)/shard_map/pallas_call | solution.py:708

commit v3 on v2

--- a/solution.py
+++ b/solution.py
@@ -18,12 +18,12 @@
 ORDER = tuple(first + n for first, size in RUNS for n in range(size))
 PLACE = tuple(ORDER.index(field) for field in range(len(ORDER)))
 MIXED = (17, 18, 19, 20, 0)
-SIZES = (1, 4, 3, 3, 2, 4, 4, 4)
+SIZES = (1, 4, 3, 3, 1, 4, 5, 4)
 STAGES = len(SIZES)
 FIRST = tuple(sum(SIZES[:s]) for s in range(STAGES + 1))
 MIX_STAGE = 4
 TURNED = 3
-TURN_LAG = 6
+FINAL = 0
 Y_GROUPS = ((0, 1), (1, 2), (2, STAGES))
 PAD = 8
 
@@ -228,12 +228,11 @@
         gauges.append(gauge)
         emit(14 + one, advected[14 + one] + gauge)
 
-    connection_rate(0)
     yield
 
     begin(5)
-    connection_rate(1)
-    connection_rate(2)
+    for one in range(3):
+        connection_rate(one)
     ricci = []
     for k, (one, two) in enumerate(PAIR_LIST):
         conf = second(0, one, two)
@@ -262,11 +261,10 @@
         )
 
     traceless_rate(0)
-    traceless_rate(1)
     yield
 
     begin(6)
-    for k in range(2, 6):
+    for k in range(1, 6):
         traceless_rate(k)
     yield
 
@@ -284,7 +282,7 @@
 
 def section_kernel(
     sizes, section, base, accum, ns_out, na_out, slab,
-    xb, tb, tile, bb, ab, local_sem, halo_send, halo_recv,
+    xb, tb, eb, tile, bb, ab, local_sem, halo_send, halo_recv,
     line_send, gather_recv,
 ):
     gx, gy, gz = sizes
@@ -313,10 +311,11 @@
         ).wait_send()
 
     own_planes, own_rows = pl.ds(2, planes), pl.ds(PAD, rows)
-    SENT = dict(z=0, y=1, yz=2, x=3, xy=4, xz=5)
+    SENT = dict(z=0, y=1, yz=2, x=3, xy=4, xz=5, ze=6)
     GOT_Z, GOT_Y = 0, STAGES
     GOT_YZ = STAGES + len(Y_GROUPS)
-    GOT_X, GOT_XY, GOT_XZ = GOT_YZ + 1, GOT_YZ + 2, GOT_YZ + 3
+    GOT_X, GOT_XY, GOT_XZ, GOT_ZE = (GOT_YZ + n for n in (1, 2, 3, 4))
+    mixed = pl.ds(0, len(MIXED))
 
     def halo(delta, kind, got, src, dst):
         return pltpu.make_async_remote_copy(
@@ -354,11 +353,23 @@
             xb.at[run, own_planes, src, :], xb.at[run, own_planes, dst, :],
         )
 
+    def z_edge(dz, dy):
+        src, _ = planes_of(dz)
+        cut, _ = rows_of(dy)
+        place = pl.ds(0 if dz == 1 else 2, 2), pl.ds(0 if dy == 1 else 2, 2)
+        return halo(
+            (0, 0, dz), "ze", GOT_ZE,
+            xb.at[mixed, src, cut, :], eb.at[mixed, place[0], place[1], :],
+        )
+
     def yz_edge(dy, side):
-        run = pl.ds(0, len(MIXED))
-        src, dst = rows_of(dy)
+        _, dst = rows_of(dy)
         cut = pl.ds(0, 2) if side == 0 else pl.ds(2 + planes, 2)
-        return halo((0, dy, 0), "yz", GOT_YZ, xb.at[run, cut, src, :], xb.at[run, cut, dst, :])
+        return halo(
+            (0, dy, 0), "yz", GOT_YZ,
+            eb.at[mixed, pl.ds(2 * side, 2), pl.ds(0 if dy == 1 else 2, 2), :],
+            xb.at[mixed, cut, dst, :],
+        )
 
     def xy_edge(slot, dy):
         src, dst = rows_of(dy)
@@ -377,6 +388,7 @@
     steps, slots = (1, -1), range(len(x_steps))
     z_faces = [[z_face(s, dz) for dz in steps] for s in range(STAGES)]
     y_faces = [[y_face(g, dy) for dy in steps] for g in range(len(Y_GROUPS))]
+    z_edges = [z_edge(dz, dy) for dz in steps for dy in steps]
     yz_edges = [yz_edge(dy, side) for dy in steps for side in (0, 1)]
     x_faces = [
         halo((dx, 0, 0), "x", GOT_X, tile.at[0], tb.at[slot, own_planes, own_rows, :])
@@ -397,14 +409,15 @@
         landed(halo_recv.at[GOT_X], tb.at[every, own_planes, own_rows, :])
 
     def edges_landed():
-        landed(halo_recv.at[GOT_YZ], xb.at[pl.ds(0, len(MIXED)), pl.ds(0, 4), pl.ds(0, 4), :])
+        landed(halo_recv.at[GOT_YZ], xb.at[mixed, pl.ds(0, 4), pl.ds(0, 4), :])
         landed(halo_recv.at[GOT_XY], tb.at[every, own_planes, pl.ds(0, 4), :])
         landed(halo_recv.at[GOT_XZ], tb.at[every, pl.ds(0, 4), own_rows, :])
 
     def halos_left():
         left(halo_send.at[SENT["z"]], slab.at[:, pl.ds(0, 2), pl.ds(0, 2 * rows), pl.ds(0, lanes)])
         left(halo_send.at[SENT["y"]], xb.at[:, own_planes, pl.ds(0, 4), :])
-        left(halo_send.at[SENT["yz"]], xb.at[pl.ds(0, len(MIXED)), pl.ds(0, 4), pl.ds(0, 4), :])
+        left(halo_send.at[SENT["ze"]], xb.at[mixed, pl.ds(0, 4), pl.ds(0, 4), :])
+        left(halo_send.at[SENT["yz"]], xb.at[mixed, pl.ds(0, 4), pl.ds(0, 4), :])
         left(halo_send.at[SENT["x"]], tb.at[every, own_planes, own_rows, :])
         left(halo_send.at[SENT["xy"]], tb.at[every, own_planes, pl.ds(0, 4), :])
         left(halo_send.at[SENT["xz"]], tb.at[every, pl.ds(0, 4), own_rows, :])
@@ -446,7 +459,7 @@
             packed = jnp.where((lane >> 2) == field, ends, packed)
         tile[0, plane] = packed
     pl.semaphore_wait(barrier, len(partners))
-    start(z_faces[0] + y_faces[0] + x_faces)
+    start(z_faces[0] + y_faces[0] + x_faces + z_edges)
     start(z_faces[1] + y_faces[1] + z_faces[2] + y_faces[2] + z_faces[3])
     load_base.wait()
     load_accum.wait()
@@ -459,7 +472,7 @@
     pair = j + 1 - 2 * lax.rem(j, 2)
     other = 1 - i
     towards = ((0, 1), (0, -1), (1, 0), (-1, 0))
-    TURN, BULK, BULK_TURNED, PAIR_TURNED = (gy * STAGES + n for n in (0, turned, turned + 1, turned + 2))
+    TURN, BULK, BULK_TURNED, PAIR_TURNED = ((gy - 1) * STAGES + n for n in (0, turned, turned + 1, turned + 2))
     SENT_PAIR, SENT_TURNED = 4, 5
 
     def piece(bi, bj, low, high):
@@ -482,14 +495,16 @@
             device_id_type=MESH,
         ).start()
 
-    def number(bi, bj, c):
-        return (bj if paired else bi * gy + bj) * STAGES + c
+    def number(link, bi, bj, c):
+        if paired:
+            return (bj - link) * STAGES + c
+        return (bi * gy + bj) * STAGES + c
 
     def send(link, bi, bj, c):
-        line(link, bi, bj, c, link, number(bi, bj, c))
-
-    def arrive(bi, bj, c):
-        landed(gather_recv.at[number(bi, bj, c)], piece(bi, bj, c, c + 1))
+        line(link, bi, bj, c, link, number(link, bi, bj, c))
+
+    def arrive(link, bi, bj, c):
+        landed(gather_recv.at[number(link, bi, bj, c)], piece(bi, bj, c, c + 1))
 
     def x_links(body):
         @pl.when(i + 1 < gx)
@@ -515,22 +530,38 @@
         else:
             line(2, i, bj, c, 2, BULK_TURNED)
 
+    def held(c, ahead):
+        if c < kept:
+            return False
+        return (pair == j + ahead) & ((pair == 0) | (pair == gy - 1))
+
     def send_own(c):
-        @pl.when(j + 1 < gy)
+        @pl.when((j + 1 < gy) & jnp.logical_not(held(c, 1)))
         def _():
             send(0, i, j, c)
 
-        @pl.when(j > 0)
+        @pl.when((j > 0) & jnp.logical_not(held(c, -1)))
         def _():
             send(1, i, j, c)
 
         cross(j, c, 0)
 
+    def send_held(c):
+        def go(link, ahead):
+            pl.when(held(c, ahead))(
+                lambda: line(link, i, j, c, link, number(link, i, j, kept))
+            )
+
+        go(0, 1)
+        go(1, -1)
+
     def pass_on(d, c):
-        @pl.when(j - d >= 0)
+        ended = d == 1 and c >= kept
+
+        @pl.when((j - d >= 0) & (j + 1 < gy) if ended else j - d >= 0)
         def _():
             bj = j - d
-            arrive(i, bj, c)
+            arrive(0, i, bj, c)
 
             @pl.when(j + 1 < gy)
             def _():
@@ -538,10 +569,10 @@
 
             cross(bj, c, d)
 
-        @pl.when(j + d < gy)
+        @pl.when((j + d < gy) & (j > 0) if ended else j + d < gy)
         def _():
             bj = j + d
-            arrive(i, bj, c)
+            arrive(1, i, bj, c)
 
             @pl.when(j > 0)
             def _():
@@ -582,7 +613,8 @@
     def own_stage(s):
         if s:
             z_landed(s)
-        if s == 1:
+        else:
+            landed(halo_recv.at[GOT_ZE], eb.at[mixed, pl.ds(0, 4), pl.ds(0, 4), :])
             start(yz_edges)
         if s < len(Y_GROUPS):
             y_landed(s)
@@ -592,15 +624,20 @@
             next(part)
         send_own(s)
 
-    LAG = tuple(1 + 2 * d for d in range(gy))
-    for v in range(STAGES + max(LAG)):
+    LAG = tuple(3 * d for d in range(gy))
+    final = STAGES - 1 + LAG[gy - 2] + FINAL
+    for v in range(STAGES + LAG[gy - 1]):
         if v < STAGES:
             own_stage(v)
         for d in range(1, gy):
             if 0 <= v - LAG[d] < STAGES:
                 pass_on(d, v - LAG[d])
-        if kept <= v - TURN_LAG < STAGES:
-            turn(v - TURN_LAG)
+        for c in range(kept, STAGES):
+            if v == final - (c == kept):
+                send_held(c)
+        if v == final:
+            for c in range(kept, STAGES):
+                turn(c)
 
     halos_left()
 
@@ -610,6 +647,12 @@
     if paired:
         if turned:
             landed(gather_recv.at[PAIR_TURNED], whole(rows, lanes, kept))
+
+            for link, end in ((1, 0), (0, gy - 1)):
+                @pl.when(j == end)
+                def _():
+                    slot = gather_recv.at[number(link, i, pair, kept)]
+                    landed(slot, whole(rows, lanes, kept))
         landed(gather_recv.at[BULK], whole(gy * rows, lanes, 0, kept))
         if turned and gy > 2:
             landed(gather_recv.at[BULK_TURNED], whole((gy - 2) * rows, lanes, kept))
@@ -619,7 +662,7 @@
                 @pl.when(i - d >= 0)
                 def _():
                     for c in range(STAGES):
-                        arrive(i - d, bj, c)
+                        arrive(2, i - d, bj, c)
 
                         @pl.when(i + 1 < gx)
                         def _():
@@ -628,7 +671,7 @@
                 @pl.when(i + d < gx)
                 def _():
                     for c in range(STAGES):
-                        arrive(i + d, bj, c)
+                        arrive(3, i + d, bj, c)
 
                         @pl.when(i > 0)
                         def _():
@@ -681,7 +724,7 @@
     gx, gy, gz = sizes
     fields, planes, rows, lanes = section.shape
     slots = 1 if gx == 2 else 2
-    arrivals = gy * STAGES + TURNED + 3 if gx == 2 and gy % 2 == 0 else gx * gy * STAGES
+    arrivals = (gy - 1) * STAGES + TURNED + 3 if gx == 2 and gy % 2 == 0 else gx * gy * STAGES
     any_spec = pl.BlockSpec(memory_space=pl.ANY)
     block = jax.ShapeDtypeStruct(section.shape, jnp.float32)
     slab = jax.ShapeDtypeStruct((fields, planes, gy * rows, gx * lanes), jnp.float32)
@@ -694,12 +737,13 @@
         scratch_shapes=[
             pltpu.VMEM((fields, planes + 4, rows + 2 * PAD, lanes), jnp.float32),
             pltpu.VMEM((slots, planes + 4, rows + 2 * PAD, lanes), jnp.float32),
+            pltpu.VMEM((len(MIXED), 4, 8, lanes), jnp.float32),
             pltpu.VMEM((1, planes, rows, lanes), jnp.float32),
             pltpu.VMEM(section.shape, jnp.float32),
             pltpu.VMEM(section.shape, jnp.float32),
             dma((3,)),
-            dma((6,)),
-            dma((STAGES + len(Y_GROUPS) + 4,)),
+            dma((7,)),
+            dma((STAGES + len(Y_GROUPS) + 5,)),
             dma((6,)),
             dma((arrivals,)),
         ],

time: 46.3 us -> 45.4 us (0.981)
  Pallas kernels: 45.5 us -> 44.6 us
    pallas_call x1, Pallas kernels: 43.5 us -> 42.6 us  [shards(): pl.pallas_call(functools.partial(section_kernel, sizes), out_shape=tuple(...]
where the time goes in v3:
time: 45.4 us; the launch traced here: 45.3 us
  Pallas kernels  44.6 us (98%)
  between operations  0.64 us (1%)
    pallas_call x1, Pallas kernels, shards(): pl.pallas_call(functools.partial(section_kernel, sizes), out_shape=tuple(...  42.6 us
    pallas_call x1, Pallas kernels, shards(): pl.pallas_call(put_out, out_shape=(block, block, slab), in_specs=[pl.Bloc...  1.99 us

profile of v3, /device:TPU:0, one launch (start us, length us, event | category | flops | bytes accessed | tf_op | source)
XLA Modules:
  0.0 45.3 jit_solution(17341768113547807519)
XLA Ops:
  0.6 42.6 %shard_map.58 = (f32[25,2,16,128]{3,2,1,0:T(8,128)S(1)}, f32[25,2,16,128]{3,2,1,0:T(8,128)S(1)}, f32[25,2,64,256]{3,2,1,0:T(8,128)S(1)}) custom-call(f32[25,2,16,128]{3,2,1,0:T(8,128)} %section.1, f32[25,2,16,128]{3,2,1,0:T(8,128)} %base.1, f32[25,2,16,128]{3,2,1,0:T(8,128)} %accum.1), custom_call_target="tpu_custom_call" | custom-call | tf_op jit(solution)/shard_map/pallas_call | solution.py:732
  43.3 2.0 %shard_map.59 = (f32[25,2,16,128]{3,2,1,0:T(8,128)}, f32[25,2,16,128]{3,2,1,0:T(8,128)}, f32[25,2,64,256]{3,2,1,0:T(8,128)}) custom-call(f32[25,2,16,128]{3,2,1,0:T(8,128)S(1)} %get-tuple-element.6.ns_in, f32[25,2,16,128]{3,2,1,0:T(8,128)S(1)} %get-tuple-element.7.na_in, f32[25,2,64,256]{3,2,1,0:T(8,128)S(1)} %get-tuple-element.8.slab_in), custom_call_target="tpu_custom_call" | custom-call | tf_op jit(solution)/shard_map/pallas_call | solution.py:752

commit v4 on v3

--- a/solution.py
+++ b/solution.py
@@ -21,10 +21,11 @@
 SIZES = (1, 4, 3, 3, 1, 4, 5, 4)
 STAGES = len(SIZES)
 FIRST = tuple(sum(SIZES[:s]) for s in range(STAGES + 1))
-MIX_STAGE = 4
+MIX_STAGE = next(s for s in range(STAGES) if FIRST[s + 1] > PLACE[7])
 TURNED = 3
 FINAL = 0
 Y_GROUPS = ((0, 1), (1, 2), (2, STAGES))
+EARLY = 4
 PAD = 8
 
 
@@ -161,129 +162,112 @@
             total = term if total is None else total + term
         return total
 
-    def begin(stage):
-        for field in ORDER[FIRST[stage] : FIRST[stage + 1]]:
-            differentiate(field)
-
     chi, trace, lapse, theta = centre[0], centre[7], centre[17], centre[24]
-
-    begin(0)
-    emit(17, advected[17] - 2.0 * lapse * (trace - 2.0 * theta))
-    yield
-
-    begin(1)
-    div = grad[18][0] + grad[19][1] + grad[20][2]
-    third_div = (2.0 / 3.0) * div
-    for one in range(3):
-        emit(18 + one, advected[18 + one] + 0.75 * centre[21 + one])
-    emit(0, advected[0] + (2.0 / 3.0) * chi * (lapse * trace) - chi * third_div)
-    yield
-
-    def metric_rate(k):
+    shared, gauges = {}, {}
+
+    def once(name, make):
+        if name not in shared:
+            shared[name] = make()
+        return shared[name]
+
+    def third_div():
+        div = grad[18][0] + grad[19][1] + grad[20][2]
+        return (2.0 / 3.0) * div
+
+    def lapse_terms():
+        mix()
+        lapse_dd = [second(17, one, two) for one, two in PAIR_LIST]
+        return lapse_dd, contract(inverse, lapse_dd)
+
+    def ricci_terms():
+        half_over = 0.5 * once("over", lambda: 1.0 / chi)
+        ricci = []
+        for k, (one, two) in enumerate(PAIR_LIST):
+            conf = second(0, one, two)
+            if one == two:
+                conf = conf + lap[0]
+                grads_g = grad[14 + one][one]
+            else:
+                grads_g = 0.5 * (grad[14 + two][one] + grad[14 + one][two])
+            ricci.append(-0.5 * lap[1 + k] + grads_g + conf * half_over)
+        return ricci, contract(inverse, ricci)
+
+    def rate_of(field):
+        rate = advected[field]
+        if field == 17:
+            return rate - 2.0 * lapse * (trace - 2.0 * theta)
+        third = once("div", third_div)
+        if field in (18, 19, 20):
+            return rate + 0.75 * centre[field + 3]
+        if field == 0:
+            return rate + (2.0 / 3.0) * chi * (lapse * trace) - chi * third
+        if field in range(1, 7):
+            k = field - 1
+            one, two = PAIR_LIST[k]
+            lie = lie_of(metric, one, two)
+            return rate - 2.0 * lapse * traceless[k] + lie - metric[k] * third
+        lapse_dd, lapse_trace = once("lapse", lapse_terms)
+        squares = once("squares", lambda: contract(traceless, traceless))
+        if field == 7:
+            return (
+                rate
+                - chi * lapse_trace
+                + lapse * (squares + trace * trace * (1.0 / 3.0))
+                + KAPPA_ONE * lapse * theta
+            )
+        if field in (14, 15, 16):
+            one = field - 14
+            a_lapse = sum(sym(traceless, one, k) * grad[17][k] for k in range(3))
+            a_chi = sum(sym(traceless, one, k) * grad[0][k] for k in range(3))
+            g_trace = sum(sym(inverse, one, k) * grad[7][k] for k in range(3))
+            b_mixed = sum(second(18 + k, one, k) for k in range(3))
+            g_shift = sum(centre[14 + k] * grad[18 + one][k] for k in range(3))
+            over_chi = once("over", lambda: 1.0 / chi)
+            gauges[one] = (
+                -2.0 * a_lapse
+                - lapse * ((4.0 / 3.0) * g_trace + 3.0 * (a_chi * over_chi))
+                + lap[18 + one]
+                + b_mixed * (1.0 / 3.0)
+                + centre[14 + one] * third
+                - g_shift
+            )
+            return rate + gauges[one]
+        if field in (21, 22, 23):
+            return rate + gauges[field - 21] - DRIVER_ETA * centre[field]
+        ricci, ricci_trace = once("ricci", ricci_terms)
+        if field == 24:
+            return (
+                rate
+                + 0.5 * lapse * (chi * ricci_trace + (2.0 / 3.0) * trace * trace - squares)
+                - 2.0 * KAPPA_ONE * lapse * theta
+            )
+        k = field - 8
         one, two = PAIR_LIST[k]
-        emit(
-            1 + k,
-            advected[1 + k]
-            - 2.0 * lapse * traceless[k]
-            + lie_of(metric, one, two)
-            - metric[k] * third_div,
-        )
-
-    for stage in (2, 3):
-        begin(stage)
-        for field in ORDER[FIRST[stage] : FIRST[stage + 1]]:
-            metric_rate(field - 1)
-        yield
-
-    begin(4)
-    mix()
-    over_chi = 1.0 / chi
-    half_over = 0.5 * over_chi
-    squares = contract(traceless, traceless)
-    lapse_dd = [second(17, one, two) for one, two in PAIR_LIST]
-    lapse_trace = contract(inverse, lapse_dd)
-    emit(
-        7,
-        advected[7]
-        - chi * lapse_trace
-        + lapse * (squares + trace * trace * (1.0 / 3.0))
-        + KAPPA_ONE * lapse * theta,
-    )
-    gauges = []
-
-    def connection_rate(one):
-        a_lapse = sum(sym(traceless, one, k) * grad[17][k] for k in range(3))
-        a_chi = sum(sym(traceless, one, k) * grad[0][k] for k in range(3))
-        g_trace = sum(sym(inverse, one, k) * grad[7][k] for k in range(3))
-        b_mixed = sum(second(18 + k, one, k) for k in range(3))
-        g_shift = sum(centre[14 + k] * grad[18 + one][k] for k in range(3))
-        gauge = (
-            -2.0 * a_lapse
-            - lapse * ((4.0 / 3.0) * g_trace + 3.0 * (a_chi * over_chi))
-            + lap[18 + one]
-            + b_mixed * (1.0 / 3.0)
-            + centre[14 + one] * third_div
-            - g_shift
-        )
-        gauges.append(gauge)
-        emit(14 + one, advected[14 + one] + gauge)
-
-    yield
-
-    begin(5)
-    for one in range(3):
-        connection_rate(one)
-    ricci = []
-    for k, (one, two) in enumerate(PAIR_LIST):
-        conf = second(0, one, two)
-        if one == two:
-            conf = conf + lap[0]
-            grads_g = grad[14 + one][one]
-        else:
-            grads_g = 0.5 * (grad[14 + two][one] + grad[14 + one][two])
-        ricci.append(-0.5 * lap[1 + k] + grads_g + conf * half_over)
-    ricci_trace = contract(inverse, ricci)
-    third_trace = (lapse * ricci_trace - lapse_trace) * (1.0 / 3.0)
-
-    def traceless_rate(k):
-        one, two = PAIR_LIST[k]
+        third_trace = once("trace", lambda: (lapse * ricci_trace - lapse_trace) * (1.0 / 3.0))
         free = lapse * ricci[k] - lapse_dd[k] - metric[k] * third_trace
         product = sum(
             sym(traceless, one, m) * sym(traceless, m, two) for m in range(3)
         )
-        emit(
-            8 + k,
-            advected[8 + k]
+        return (
+            rate
             + chi * free
             + lapse * (trace * traceless[k] - 2.0 * product)
             + lie_of(traceless, one, two)
-            - traceless[k] * third_div,
-        )
-
-    traceless_rate(0)
-    yield
-
-    begin(6)
-    for k in range(1, 6):
-        traceless_rate(k)
-    yield
-
-    begin(7)
-    for one in range(3):
-        emit(21 + one, advected[21 + one] + gauges[one] - DRIVER_ETA * centre[21 + one])
-    emit(
-        24,
-        advected[24]
-        + 0.5 * lapse * (chi * ricci_trace + (2.0 / 3.0) * trace * trace - squares)
-        - 2.0 * KAPPA_ONE * lapse * theta,
-    )
-    yield
+            - traceless[k] * third
+        )
+
+    for stage in range(STAGES):
+        for field in ORDER[FIRST[stage] : FIRST[stage + 1]]:
+            differentiate(field)
+        for field in ORDER[FIRST[stage] : FIRST[stage + 1]]:
+            emit(field, rate_of(field))
+        yield
 
 
 def section_kernel(
     sizes, section, base, accum, ns_out, na_out, slab,
     xb, tb, eb, tile, bb, ab, local_sem, halo_send, halo_recv,
-    line_send, gather_recv,
+    line_send, gather_recv, chain,
 ):
     gx, gy, gz = sizes
     fields, planes, rows, lanes = section.shape
@@ -439,11 +423,20 @@
         place += size
     load_base = pltpu.make_async_copy(base, bb, local_sem.at[1])
     load_accum = pltpu.make_async_copy(accum, ab, local_sem.at[2])
-    partners = [(0, 0, 1), (0, 0, -1)] + [(dx, 0, 0) for dx in x_steps] + [(0, 1, 0), (0, -1, 0)]
+    chained = gy > 2
+    faces = [(0, 0, 1), (0, 0, -1)] + [(dx, 0, 0) for dx in x_steps]
+    barrier = pltpu.get_barrier_semaphore()
+
+    def greet(sem, delta):
+        pl.semaphore_signal(sem, inc=1, device_id=device(*delta), device_id_type=MESH)
+
+    for delta in faces + [(0, -1, 0)]:
+        greet(barrier, delta)
+    if chained:
+        pl.when(j + 1 < gy)(lambda: greet(barrier, (0, 1, 0)))
+    else:
+        greet(barrier, (0, 1, 0))
     start(loads)
-    barrier = pltpu.get_barrier_semaphore()
-    for delta in partners:
-        pl.semaphore_signal(barrier, inc=1, device_id=device(*delta), device_id_type=MESH)
     load_base.start()
     load_accum.start()
 
@@ -458,9 +451,39 @@
             ends = pltpu.roll(value, (4 * field + 2) % lanes, 1)
             packed = jnp.where((lane >> 2) == field, ends, packed)
         tile[0, plane] = packed
-    pl.semaphore_wait(barrier, len(partners))
-    start(z_faces[0] + y_faces[0] + x_faces + z_edges)
-    start(z_faces[1] + y_faces[1] + z_faces[2] + y_faces[2] + z_faces[3])
+    if chained:
+        pl.when(j == 0)(lambda: pl.semaphore_wait(barrier, len(faces) + 1))
+        pl.when(j > 0)(lambda: pl.semaphore_wait(barrier, len(faces) + 2))
+    else:
+        pl.semaphore_wait(barrier, len(faces) + 2)
+    def far(some):
+        pl.when(j == 0)(lambda: start(some))
+
+    def near(some):
+        up, down = some[::2], some[1::2]
+        start(up)
+        pl.when(j > 0)(lambda: start(down))
+
+    if not chained:
+        near = start
+    else:
+        pl.when(j == gy - 2)(lambda: greet(chain, (0, -1, 0)))
+    start(z_faces[0])
+    near(y_faces[0])
+    start(x_faces + z_edges + z_faces[1])
+    near(y_faces[1])
+    start(z_faces[2])
+    near(y_faces[2])
+    for s in range(3, EARLY):
+        start(z_faces[s])
+    if chained:
+        @pl.when(j < gy - 2)
+        def _():
+            pl.semaphore_wait(chain, 1)
+            pl.when(j > 0)(lambda: greet(chain, (0, -1, 0)))
+
+        for faces_of in y_faces:
+            far(faces_of[1::2])
     load_base.wait()
     load_accum.wait()
 
@@ -602,7 +625,7 @@
 
     x_landed()
     start(xz_edges + xy_edges)
-    for s in range(4, STAGES):
+    for s in range(EARLY, STAGES):
         start(z_faces[s])
     z_landed(0)
     work = [
@@ -746,6 +769,7 @@
             dma((STAGES + len(Y_GROUPS) + 5,)),
             dma((6,)),
             dma((arrivals,)),
+            pltpu.SemaphoreType.REGULAR,
         ],
         compiler_params=pltpu.CompilerParams(collective_id=0, has_side_effects=True, vmem_limit_bytes=24 << 20),
     )(*(pltpu.with_memory_space_constraint(x, pltpu.HBM) for x in (section, base, accum)))

time: 45.4 us -> 44.8 us (0.987)
  Pallas kernels: 44.6 us -> 44 us
    pallas_call x1, Pallas kernels: 42.6 us -> 42 us  [shards(): pl.pallas_call(functools.partial(section_kernel, sizes), out_shape=tuple(...]
where the time goes in v4:
time: 44.8 us; the launch traced here: 44.6 us
  Pallas kernels  44 us (98%)
  between operations  0.64 us (1%)
    pallas_call x1, Pallas kernels, shards(): pl.pallas_call(functools.partial(section_kernel, sizes), out_shape=tuple(...  42 us
    pallas_call x1, Pallas kernels, shards(): pl.pallas_call(put_out, out_shape=(block, block, slab), in_specs=[pl.Bloc...  1.99 us

profile of v4, /device:TPU:0, one launch (start us, length us, event | category | flops | bytes accessed | tf_op | source)
XLA Modules:
  0.0 44.6 jit_solution(10215382572554153200)
XLA Ops:
  0.6 42.0 %shard_map.58 = (f32[25,2,16,128]{3,2,1,0:T(8,128)S(1)}, f32[25,2,16,128]{3,2,1,0:T(8,128)S(1)}, f32[25,2,64,256]{3,2,1,0:T(8,128)S(1)}) custom-call(f32[25,2,16,128]{3,2,1,0:T(8,128)} %section.1, f32[25,2,16,128]{3,2,1,0:T(8,128)} %base.1, f32[25,2,16,128]{3,2,1,0:T(8,128)} %accum.1), custom_call_target="tpu_custom_call" | custom-call | tf_op jit(solution)/shard_map/pallas_call | solution.py:755
  42.6 2.0 %shard_map.59 = (f32[25,2,16,128]{3,2,1,0:T(8,128)}, f32[25,2,16,128]{3,2,1,0:T(8,128)}, f32[25,2,64,256]{3,2,1,0:T(8,128)}) custom-call(f32[25,2,16,128]{3,2,1,0:T(8,128)S(1)} %get-tuple-element.6.ns_in, f32[25,2,16,128]{3,2,1,0:T(8,128)S(1)} %get-tuple-element.7.na_in, f32[25,2,64,256]{3,2,1,0:T(8,128)S(1)} %get-tuple-element.8.slab_in), custom_call_target="tpu_custom_call" | custom-call | tf_op jit(solution)/shard_map/pallas_call | solution.py:776

commit v5 on v4

--- a/solution.py
+++ b/solution.py
@@ -14,10 +14,11 @@
 PAIR_SLOT = ((0, 1, 2), (1, 3, 4), (2, 4, 5))
 PAIR_LIST = ((0, 0), (0, 1), (0, 2), (1, 1), (1, 2), (2, 2))
 MESH = pl.DeviceIdType.MESH
-RUNS = ((17, 4), (0, 8), (14, 3), (8, 6), (21, 4))
+RUNS = ((17, 1), (19, 2), (0, 1), (18, 1), (1, 7), (14, 3), (8, 6), (21, 4))
 ORDER = tuple(first + n for first, size in RUNS for n in range(size))
 PLACE = tuple(ORDER.index(field) for field in range(len(ORDER)))
-MIXED = (17, 18, 19, 20, 0)
+MIXED = (17, 19, 20, 0, 18)
+MIXED_YZ = 4
 SIZES = (1, 4, 3, 3, 1, 4, 5, 4)
 STAGES = len(SIZES)
 FIRST = tuple(sum(SIZES[:s]) for s in range(STAGES + 1))
@@ -196,9 +197,9 @@
         rate = advected[field]
         if field == 17:
             return rate - 2.0 * lapse * (trace - 2.0 * theta)
-        third = once("div", third_div)
         if field in (18, 19, 20):
             return rate + 0.75 * centre[field + 3]
+        third = once("div", third_div)
         if field == 0:
             return rate + (2.0 / 3.0) * chi * (lapse * trace) - chi * third
         if field in range(1, 7):
@@ -266,7 +267,7 @@
 
 def section_kernel(
     sizes, section, base, accum, ns_out, na_out, slab,
-    xb, tb, eb, tile, bb, ab, local_sem, halo_send, halo_recv,
+    xb, tb, eb, tile, inputs, local_sem, halo_send, halo_recv,
     line_send, gather_recv, chain,
 ):
     gx, gy, gz = sizes
@@ -295,11 +296,11 @@
         ).wait_send()
 
     own_planes, own_rows = pl.ds(2, planes), pl.ds(PAD, rows)
-    SENT = dict(z=0, y=1, yz=2, x=3, xy=4, xz=5, ze=6)
+    SENT = dict(z=0, y=0, yz=1, ze=1, x=2, xy=2, xz=2)
     GOT_Z, GOT_Y = 0, STAGES
     GOT_YZ = STAGES + len(Y_GROUPS)
     GOT_X, GOT_XY, GOT_XZ, GOT_ZE = (GOT_YZ + n for n in (1, 2, 3, 4))
-    mixed = pl.ds(0, len(MIXED))
+    mixed = pl.ds(0, MIXED_YZ)
 
     def halo(delta, kind, got, src, dst):
         return pltpu.make_async_remote_copy(
@@ -398,13 +399,10 @@
         landed(halo_recv.at[GOT_XZ], tb.at[every, pl.ds(0, 4), own_rows, :])
 
     def halos_left():
-        left(halo_send.at[SENT["z"]], slab.at[:, pl.ds(0, 2), pl.ds(0, 2 * rows), pl.ds(0, lanes)])
-        left(halo_send.at[SENT["y"]], xb.at[:, own_planes, pl.ds(0, 4), :])
-        left(halo_send.at[SENT["ze"]], xb.at[mixed, pl.ds(0, 4), pl.ds(0, 4), :])
-        left(halo_send.at[SENT["yz"]], xb.at[mixed, pl.ds(0, 4), pl.ds(0, 4), :])
-        left(halo_send.at[SENT["x"]], tb.at[every, own_planes, own_rows, :])
-        left(halo_send.at[SENT["xy"]], tb.at[every, own_planes, pl.ds(0, 4), :])
-        left(halo_send.at[SENT["xz"]], tb.at[every, pl.ds(0, 4), own_rows, :])
+        left(halo_send.at[SENT["z"]], xb.at[:, pl.ds(0, 4), pl.ds(0, rows + planes), :])
+        left(halo_send.at[SENT["yz"]], xb.at[mixed, pl.ds(0, 4), pl.ds(0, 8), :])
+        tiles = tb.at[every, pl.ds(0, 4), pl.ds(0, planes * rows // 4 + planes + rows), :]
+        left(halo_send.at[SENT["x"]], tiles)
 
     def start(some):
         for copy in some:
@@ -421,8 +419,8 @@
             )
         )
         place += size
-    load_base = pltpu.make_async_copy(base, bb, local_sem.at[1])
-    load_accum = pltpu.make_async_copy(accum, ab, local_sem.at[2])
+    load_base = pltpu.make_async_copy(base, inputs.at[0], local_sem.at[1])
+    load_accum = pltpu.make_async_copy(accum, inputs.at[1], local_sem.at[1])
     chained = gy > 2
     faces = [(0, 0, 1), (0, 0, -1)] + [(dx, 0, 0) for dx in x_steps]
     barrier = pltpu.get_barrier_semaphore()
@@ -484,8 +482,7 @@
 
         for faces_of in y_faces:
             far(faces_of[1::2])
-    load_base.wait()
-    load_accum.wait()
+    pltpu.make_async_copy(inputs, inputs, local_sem.at[1]).wait()
 
     own_y = pl.ds(pl.multiple_of(j * rows, rows), rows)
     own_x = pl.ds(pl.multiple_of(i * lanes, lanes), lanes)
@@ -495,8 +492,8 @@
     pair = j + 1 - 2 * lax.rem(j, 2)
     other = 1 - i
     towards = ((0, 1), (0, -1), (1, 0), (-1, 0))
-    TURN, BULK, BULK_TURNED, PAIR_TURNED = ((gy - 1) * STAGES + n for n in (0, turned, turned + 1, turned + 2))
-    SENT_PAIR, SENT_TURNED = 4, 5
+    TURN, BULK, BULK_TURNED, PAIR_TURNED = ((gy - 1) * STAGES + n for n in range(4))
+    SENT_PAIR, SENT_TURNED = 3, 4
 
     def piece(bi, bj, low, high):
         return slab.at[
@@ -547,7 +544,7 @@
             else:
                 line(2, i, bj, c, 2, BULK)
         elif distance == 0:
-            line(2, i, bj, c, 2, TURN + c - kept)
+            line(2, i, bj, c, 2, TURN)
         elif distance == 1:
             pl.when(bj != pair)(lambda: line(2, i, bj, c, 2, BULK_TURNED))
         else:
@@ -603,23 +600,23 @@
 
             cross(bj, c, d)
 
-    def turn(c):
-        landed(gather_recv.at[TURN + c - kept], piece(other, j, c, c + 1))
-
-        @pl.when(pair > j)
-        def _():
-            line(0, other, j, c, SENT_TURNED, PAIR_TURNED)
-
-        @pl.when(pair < j)
-        def _():
-            line(1, other, j, c, SENT_TURNED, PAIR_TURNED)
+    def turn():
+        landed(gather_recv.at[TURN], piece(other, j, kept, STAGES))
+        for c in range(kept, STAGES):
+            @pl.when(pair > j)
+            def _():
+                line(0, other, j, c, SENT_TURNED, PAIR_TURNED)
+
+            @pl.when(pair < j)
+            def _():
+                line(1, other, j, c, SENT_TURNED, PAIR_TURNED)
 
     def emit_at(plane):
         def emit(field, rate):
-            moved = bb[field, plane] + (0.5 * STEP_DT) * rate
+            moved = inputs[0, field, plane] + (0.5 * STEP_DT) * rate
             slab[PLACE[field], plane, own_y, own_x] = moved
             ns_out[field, plane] = moved
-            na_out[field, plane] = ab[field, plane] + (STEP_DT / 3.0) * rate
+            na_out[field, plane] = inputs[1, field, plane] + (STEP_DT / 3.0) * rate
 
         return emit
 
@@ -658,9 +655,8 @@
         for c in range(kept, STAGES):
             if v == final - (c == kept):
                 send_held(c)
-        if v == final:
-            for c in range(kept, STAGES):
-                turn(c)
+        if v == final and turned:
+            turn()
 
     halos_left()
 
@@ -747,7 +743,7 @@
     gx, gy, gz = sizes
     fields, planes, rows, lanes = section.shape
     slots = 1 if gx == 2 else 2
-    arrivals = (gy - 1) * STAGES + TURNED + 3 if gx == 2 and gy % 2 == 0 else gx * gy * STAGES
+    arrivals = (gy - 1) * STAGES + 4 if gx == 2 and gy % 2 == 0 else gx * gy * STAGES
     any_spec = pl.BlockSpec(memory_space=pl.ANY)
     block = jax.ShapeDtypeStruct(section.shape, jnp.float32)
     slab = jax.ShapeDtypeStruct((fields, planes, gy * rows, gx * lanes), jnp.float32)
@@ -760,14 +756,13 @@
         scratch_shapes=[
             pltpu.VMEM((fields, planes + 4, rows + 2 * PAD, lanes), jnp.float32),
             pltpu.VMEM((slots, planes + 4, rows + 2 * PAD, lanes), jnp.float32),
-            pltpu.VMEM((len(MIXED), 4, 8, lanes), jnp.float32),
+            pltpu.VMEM((MIXED_YZ, 4, 8, lanes), jnp.float32),
             pltpu.VMEM((1, planes, rows, lanes), jnp.float32),
-            pltpu.VMEM(section.shape, jnp.float32),
-            pltpu.VMEM(section.shape, jnp.float32),
+            pltpu.VMEM((2,) + section.shape, jnp.float32),
+            dma((2,)),
             dma((3,)),
-            dma((7,)),
             dma((STAGES + len(Y_GROUPS) + 5,)),
-            dma((6,)),
+            dma((5,)),
             dma((arrivals,)),
             pltpu.SemaphoreType.REGULAR,
         ],

time: 44.8 us -> 44.6 us (level)
  no operation moved by 1% of the time
where the time goes in v5:
time: 44.6 us; the launch traced here: 44.4 us
  Pallas kernels  43.8 us (98%)
  between operations  0.64 us (1%)
    pallas_call x1, Pallas kernels, shards(): pl.pallas_call(functools.partial(section_kernel, sizes), out_shape=tuple(...  41.8 us
    pallas_call x1, Pallas kernels, shards(): pl.pallas_call(put_out, out_shape=(block, block, slab), in_specs=[pl.Bloc...  1.99 us

profile of v5, /device:TPU:0, one launch (start us, length us, event | category | flops | bytes accessed | tf_op | source)
XLA Modules:
  0.0 44.4 jit_solution(15646390146275831314)
XLA Ops:
  0.6 41.8 %shard_map.58 = (f32[25,2,16,128]{3,2,1,0:T(8,128)S(1)}, f32[25,2,16,128]{3,2,1,0:T(8,128)S(1)}, f32[25,2,64,256]{3,2,1,0:T(8,128)S(1)}) custom-call(f32[25,2,16,128]{3,2,1,0:T(8,128)} %section.1, f32[25,2,16,128]{3,2,1,0:T(8,128)} %base.1, f32[25,2,16,128]{3,2,1,0:T(8,128)} %accum.1), custom_call_target="tpu_custom_call" | custom-call | tf_op jit(solution)/shard_map/pallas_call | solution.py:751
  42.5 2.0 %shard_map.59 = (f32[25,2,16,128]{3,2,1,0:T(8,128)}, f32[25,2,16,128]{3,2,1,0:T(8,128)}, f32[25,2,64,256]{3,2,1,0:T(8,128)}) custom-call(f32[25,2,16,128]{3,2,1,0:T(8,128)S(1)} %get-tuple-element.6.ns_in, f32[25,2,16,128]{3,2,1,0:T(8,128)S(1)} %get-tuple-element.7.na_in, f32[25,2,64,256]{3,2,1,0:T(8,128)S(1)} %get-tuple-element.8.slab_in), custom_call_target="tpu_custom_call" | custom-call | tf_op jit(solution)/shard_map/pallas_call | solution.py:771

commit v6 on v5

--- a/solution.py
+++ b/solution.py
@@ -575,11 +575,10 @@
         go(0, 1)
         go(1, -1)
 
-    def pass_on(d, c):
+    def pass_on(d, c, pairs=(False, True)):
         ended = d == 1 and c >= kept
 
-        @pl.when((j - d >= 0) & (j + 1 < gy) if ended else j - d >= 0)
-        def _():
+        def below():
             bj = j - d
             arrive(0, i, bj, c)
 
@@ -589,8 +588,7 @@
 
             cross(bj, c, d)
 
-        @pl.when((j + d < gy) & (j > 0) if ended else j + d < gy)
-        def _():
+        def above():
             bj = j + d
             arrive(1, i, bj, c)
 
@@ -599,6 +597,17 @@
                 send(1, i, bj, c)
 
             cross(bj, c, d)
+
+        has_below = (j - d >= 0) & (j + 1 < gy) if ended else j - d >= 0
+        has_above = (j + d < gy) & (j > 0) if ended else j + d < gy
+        if d > 1:
+            if True in pairs:
+                pl.when(has_below)(below)
+                pl.when(has_above)(above)
+            return
+        for is_pair in pairs:
+            pl.when(has_below & ((pair < j) == is_pair))(below)
+            pl.when(has_above & ((pair > j) == is_pair))(above)
 
     def turn():
         landed(gather_recv.at[TURN], piece(other, j, kept, STAGES))

time: 44.6 us -> 44.6 us (level)
  no operation moved by 1% of the time
where the time goes in v6:
time: 44.6 us; the launch traced here: 44.4 us
  Pallas kernels  43.8 us (98%)
  between operations  0.64 us (1%)
    pallas_call x1, Pallas kernels, shards(): pl.pallas_call(functools.partial(section_kernel, sizes), out_shape=tuple(...  41.8 us
    pallas_call x1, Pallas kernels, shards(): pl.pallas_call(put_out, out_shape=(block, block, slab), in_specs=[pl.Bloc...  1.99 us

profile of v6, /device:TPU:0, one launch (start us, length us, event | category | flops | bytes accessed | tf_op | source)
XLA Modules:
  0.0 44.4 jit_solution(2724731619857895243)
XLA Ops:
  0.6 41.8 %shard_map.58 = (f32[25,2,16,128]{3,2,1,0:T(8,128)S(1)}, f32[25,2,16,128]{3,2,1,0:T(8,128)S(1)}, f32[25,2,64,256]{3,2,1,0:T(8,128)S(1)}) custom-call(f32[25,2,16,128]{3,2,1,0:T(8,128)} %section.1, f32[25,2,16,128]{3,2,1,0:T(8,128)} %base.1, f32[25,2,16,128]{3,2,1,0:T(8,128)} %accum.1), custom_call_target="tpu_custom_call" | custom-call | tf_op jit(solution)/shard_map/pallas_call | solution.py:760
  42.5 2.0 %shard_map.59 = (f32[25,2,16,128]{3,2,1,0:T(8,128)}, f32[25,2,16,128]{3,2,1,0:T(8,128)}, f32[25,2,64,256]{3,2,1,0:T(8,128)}) custom-call(f32[25,2,16,128]{3,2,1,0:T(8,128)S(1)} %get-tuple-element.6.ns_in, f32[25,2,16,128]{3,2,1,0:T(8,128)S(1)} %get-tuple-element.7.na_in, f32[25,2,64,256]{3,2,1,0:T(8,128)S(1)} %get-tuple-element.8.slab_in), custom_call_target="tpu_custom_call" | custom-call | tf_op jit(solution)/shard_map/pallas_call | solution.py:780

commit v7 on v6

--- a/solution.py
+++ b/solution.py
@@ -19,6 +19,7 @@
 PLACE = tuple(ORDER.index(field) for field in range(len(ORDER)))
 MIXED = (17, 19, 20, 0, 18)
 MIXED_YZ = 4
+XZ_LANES = (68, 76, 16)
 SIZES = (1, 4, 3, 3, 1, 4, 5, 4)
 STAGES = len(SIZES)
 FIRST = tuple(sum(SIZES[:s]) for s in range(STAGES + 1))
@@ -267,7 +268,7 @@
 
 def section_kernel(
     sizes, section, base, accum, ns_out, na_out, slab,
-    xb, tb, eb, tile, inputs, local_sem, halo_send, halo_recv,
+    xb, tb, eb, pb, qb, tile, inputs, local_sem, halo_send, halo_recv,
     line_send, gather_recv, chain,
 ):
     gx, gy, gz = sizes
@@ -296,7 +297,7 @@
         ).wait_send()
 
     own_planes, own_rows = pl.ds(2, planes), pl.ds(PAD, rows)
-    SENT = dict(z=0, y=0, yz=1, ze=1, x=2, xy=2, xz=2)
+    SENT = dict(z=0, y=0, yz=1, ze=1, x=2, xy=2, xz=3)
     GOT_Z, GOT_Y = 0, STAGES
     GOT_YZ = STAGES + len(Y_GROUPS)
     GOT_X, GOT_XY, GOT_XZ, GOT_ZE = (GOT_YZ + n for n in (1, 2, 3, 4))
@@ -363,12 +364,45 @@
             tb.at[slot, own_planes, src, :], tb.at[slot, own_planes, dst, :],
         )
 
+    tiles8 = rows // 8
+    packed_rows = pl.ds(0, tiles8)
+
     def xz_edge(slot, dz):
-        src, dst = planes_of(dz)
+        cut = pl.ds(planes - 2 if dz == 1 else 0, 2)
         return halo(
             (0, 0, dz), "xz", GOT_XZ,
-            tb.at[slot, src, own_rows, :], tb.at[slot, dst, own_rows, :],
-        )
+            pb.at[slot, cut, packed_rows, :],
+            qb.at[slot, pl.ds(0 if dz == 1 else 2, 2), packed_rows, :],
+        )
+
+    lane8 = lax.broadcasted_iota(jnp.int32, (8, lanes), 1)
+    row8 = lax.broadcasted_iota(jnp.int32, (8, lanes), 0)
+    low, spare, width = XZ_LANES
+
+    def pack_edges():
+        for slot in slots:
+            for plane in range(planes):
+                for t in range(tiles8):
+                    value = tb[slot, 2 + plane, PAD + 8 * t : PAD + 8 * t + 8, :]
+                    first = (lane8 >= spare) & (lane8 < spare + 4)
+                    value = jnp.where(first, pltpu.roll(value, spare, 1), value)
+                    inside = (lane8 >= low) & (lane8 < low + width)
+                    value = jnp.where(inside, value, 0.0)
+                    value = pltpu.roll(value, 0, 1, stride=width, stride_axis=0)
+                    pb[slot, plane, t : t + 1, :] = jnp.sum(value, axis=0, keepdims=True)
+
+    def unpack_edges():
+        for slot in slots:
+            for n, plane in enumerate((0, 1, 2 + planes, 3 + planes)):
+                for t in range(tiles8):
+                    packed = jnp.broadcast_to(qb[slot, n, t : t + 1, :], (8, lanes))
+                    value = packed
+                    for row in range(1, 8):
+                        here = pltpu.roll(packed, lanes - width * row, 1)
+                        value = jnp.where(row8 == row, here, value)
+                    first = pltpu.roll(value, lanes - spare, 1)
+                    value = jnp.where(lane8 < 4, first, value)
+                    tb[slot, plane, PAD + 8 * t : PAD + 8 * t + 8, :] = value
 
     steps, slots = (1, -1), range(len(x_steps))
     z_faces = [[z_face(s, dz) for dz in steps] for s in range(STAGES)]
@@ -396,13 +430,12 @@
     def edges_landed():
         landed(halo_recv.at[GOT_YZ], xb.at[mixed, pl.ds(0, 4), pl.ds(0, 4), :])
         landed(halo_recv.at[GOT_XY], tb.at[every, own_planes, pl.ds(0, 4), :])
-        landed(halo_recv.at[GOT_XZ], tb.at[every, pl.ds(0, 4), own_rows, :])
 
     def halos_left():
         left(halo_send.at[SENT["z"]], xb.at[:, pl.ds(0, 4), pl.ds(0, rows + planes), :])
         left(halo_send.at[SENT["yz"]], xb.at[mixed, pl.ds(0, 4), pl.ds(0, 8), :])
-        tiles = tb.at[every, pl.ds(0, 4), pl.ds(0, planes * rows // 4 + planes + rows), :]
-        left(halo_send.at[SENT["x"]], tiles)
+        left(halo_send.at[SENT["x"]], tb.at[every, pl.ds(0, planes), pl.ds(0, rows + 4), :])
+        left(halo_send.at[SENT["xz"]], qb.at[every, pl.ds(0, 4), packed_rows, :])
 
     def start(some):
         for copy in some:
@@ -630,7 +663,9 @@
         return emit
 
     x_landed()
-    start(xz_edges + xy_edges)
+    start(xy_edges)
+    pack_edges()
+    start(xz_edges)
     for s in range(EARLY, STAGES):
         start(z_faces[s])
     z_landed(0)
@@ -652,6 +687,9 @@
         for part in work:
             next(part)
         send_own(s)
+        if s == MIX_STAGE - 1:
+            landed(halo_recv.at[GOT_XZ], qb.at[every, pl.ds(0, 4), packed_rows, :])
+            unpack_edges()
 
     LAG = tuple(3 * d for d in range(gy))
     final = STAGES - 1 + LAG[gy - 2] + FINAL
@@ -766,10 +804,12 @@
             pltpu.VMEM((fields, planes + 4, rows + 2 * PAD, lanes), jnp.float32),
             pltpu.VMEM((slots, planes + 4, rows + 2 * PAD, lanes), jnp.float32),
             pltpu.VMEM((MIXED_YZ, 4, 8, lanes), jnp.float32),
+            pltpu.VMEM((slots, planes, 8, lanes), jnp.float32),
+            pltpu.VMEM((slots, 4, 8, lanes), jnp.float32),
             pltpu.VMEM((1, planes, rows, lanes), jnp.float32),
             pltpu.VMEM((2,) + section.shape, jnp.float32),
             dma((2,)),
-            dma((3,)),
+            dma((4,)),
             dma((STAGES + len(Y_GROUPS) + 5,)),
             dma((5,)),
             dma((arrivals,)),

time: 44.6 us -> 44.6 us (level)
  no operation moved by 1% of the time
where the time goes in v7:
time: 44.6 us; the launch traced here: 44.5 us
  Pallas kernels  43.8 us (98%)
  between operations  0.64 us (1%)
    pallas_call x1, Pallas kernels, shards(): pl.pallas_call(functools.partial(section_kernel, sizes), out_shape=tuple(...  41.8 us
    pallas_call x1, Pallas kernels, shards(): pl.pallas_call(put_out, out_shape=(block, block, slab), in_specs=[pl.Bloc...  1.99 us

profile of v7, /device:TPU:0, one launch (start us, length us, event | category | flops | bytes accessed | tf_op | source)
XLA Modules:
  0.0 44.5 jit_solution(5535933862131157087)
XLA Ops:
  0.6 41.8 %shard_map.58 = (f32[25,2,16,128]{3,2,1,0:T(8,128)S(1)}, f32[25,2,16,128]{3,2,1,0:T(8,128)S(1)}, f32[25,2,64,256]{3,2,1,0:T(8,128)S(1)}) custom-call(f32[25,2,16,128]{3,2,1,0:T(8,128)} %section.1, f32[25,2,16,128]{3,2,1,0:T(8,128)} %base.1, f32[25,2,16,128]{3,2,1,0:T(8,128)} %accum.1), custom_call_target="tpu_custom_call" | custom-call | tf_op jit(solution)/shard_map/pallas_call | solution.py:798
  42.5 2.0 %shard_map.59 = (f32[25,2,16,128]{3,2,1,0:T(8,128)}, f32[25,2,16,128]{3,2,1,0:T(8,128)}, f32[25,2,64,256]{3,2,1,0:T(8,128)}) custom-call(f32[25,2,16,128]{3,2,1,0:T(8,128)S(1)} %get-tuple-element.6.ns_in, f32[25,2,16,128]{3,2,1,0:T(8,128)S(1)} %get-tuple-element.7.na_in, f32[25,2,64,256]{3,2,1,0:T(8,128)S(1)} %get-tuple-element.8.slab_in), custom_call_target="tpu_custom_call" | custom-call | tf_op jit(solution)/shard_map/pallas_call | solution.py:820

commit v8 on v7

--- a/solution.py
+++ b/solution.py
@@ -666,7 +666,7 @@
     start(xy_edges)
     pack_edges()
     start(xz_edges)
-    for s in range(EARLY, STAGES):
+    for s in range(EARLY, STAGES - 2):
         start(z_faces[s])
     z_landed(0)
     work = [
@@ -687,6 +687,8 @@
         for part in work:
             next(part)
         send_own(s)
+        if s < 2:
+            start(z_faces[STAGES - 2 + s])
         if s == MIX_STAGE - 1:
             landed(halo_recv.at[GOT_XZ], qb.at[every, pl.ds(0, 4), packed_rows, :])
             unpack_edges()

time: 44.6 us -> 44.6 us (level)
  no operation moved by 1% of the time
where the time goes in v8:
time: 44.6 us; the launch traced here: 44.5 us
  Pallas kernels  43.8 us (98%)
  between operations  0.64 us (1%)
    pallas_call x1, Pallas kernels, shards(): pl.pallas_call(functools.partial(section_kernel, sizes), out_shape=tuple(...  41.8 us
    pallas_call x1, Pallas kernels, shards(): pl.pallas_call(put_out, out_shape=(block, block, slab), in_specs=[pl.Bloc...  1.99 us

profile of v8, /device:TPU:0, one launch (start us, length us, event | category | flops | bytes accessed | tf_op | source)
XLA Modules:
  0.0 44.5 jit_solution(6023821897999288612)
XLA Ops:
  0.6 41.8 %shard_map.58 = (f32[25,2,16,128]{3,2,1,0:T(8,128)S(1)}, f32[25,2,16,128]{3,2,1,0:T(8,128)S(1)}, f32[25,2,64,256]{3,2,1,0:T(8,128)S(1)}) custom-call(f32[25,2,16,128]{3,2,1,0:T(8,128)} %section.1, f32[25,2,16,128]{3,2,1,0:T(8,128)} %base.1, f32[25,2,16,128]{3,2,1,0:T(8,128)} %accum.1), custom_call_target="tpu_custom_call" | custom-call | tf_op jit(solution)/shard_map/pallas_call | solution.py:800
  42.5 2.0 %shard_map.59 = (f32[25,2,16,128]{3,2,1,0:T(8,128)}, f32[25,2,16,128]{3,2,1,0:T(8,128)}, f32[25,2,64,256]{3,2,1,0:T(8,128)}) custom-call(f32[25,2,16,128]{3,2,1,0:T(8,128)S(1)} %get-tuple-element.6.ns_in, f32[25,2,16,128]{3,2,1,0:T(8,128)S(1)} %get-tuple-element.7.na_in, f32[25,2,64,256]{3,2,1,0:T(8,128)S(1)} %get-tuple-element.8.slab_in), custom_call_target="tpu_custom_call" | custom-call | tf_op jit(solution)/shard_map/pallas_call | solution.py:822
